TPU v7x, 16 devices: a 4x2x1 block of a 4x4x8 slice. The times are simulated.
16 devices in a mesh: dp: 2 (over y, z), cp: 8 (over x, core).
Axes of the slice: x: 4, y: 2, z: 1, core: 2. Of those that a mesh axis runs over, the one named last changes fastest.
The devices are a block of a 4x4x8 slice.
Arguments:
- q_tok: bfloat16 [16384, 3, 128], P(('dp', 'cp')), parts along dimension 0
- k_tok: bfloat16 [16384, 128], P(('dp', 'cp')), parts along dimension 0
- v_tok: bfloat16 [16384, 128], P(('dp', 'cp')), parts along dimension 0
- fwd_out: bfloat16 [16384, 3, 128], P(('dp', 'cp')), parts along dimension 0
- d_out: bfloat16 [16384, 3, 128], P(('dp', 'cp')), parts along dimension 0
- lse_row: float32 [16384, 3], P(('dp', 'cp')), parts along dimension 0
Outputs:
- output 1: bfloat16 [16384, 3, 128], P(('dp', 'cp')), parts along dimension 0
- output 2: bfloat16 [16384, 128], P(('dp', 'cp')), parts along dimension 0
- output 3: bfloat16 [16384, 128], P(('dp', 'cp')), parts along dimension 0
There are 2 independent parts. A program takes and returns all parts, laid end to end along the dimension named above; each array names one.
All inputs are finite; a program needn't handle non-finite values.
Results may differ from a plain program's by a relative error of at most 0.001.
Values are sent between devices in bfloat16 or wider.
A program may use at most 768 MiB of HBM per device.

v0:
```python
import jax
import jax.numpy as jnp
from jax import lax
from jax.sharding import PartitionSpec as P


def pair_scores(q_block, do_block, lse_block, delta_block, k_block, v_block, on_diag, softmax_scale):
    logits = jnp.einsum('rgd,cd->rgc', q_block, k_block, preferred_element_type=jnp.float32)
    row_ids = jnp.arange(q_block.shape[0])
    allowed = jnp.logical_or(row_ids[None, :] <= row_ids[:, None], jnp.logical_not(on_diag))
    prob_mat = jnp.exp(jnp.where(allowed[:, None, :], logits * softmax_scale - lse_block[:, :, None], -jnp.inf))
    d_prob = jnp.einsum('rgd,cd->rgc', do_block, v_block, preferred_element_type=jnp.float32)
    d_score = (prob_mat * (d_prob - delta_block[:, :, None])).astype(jnp.bfloat16)
    return prob_mat.astype(jnp.bfloat16), d_score


def solution(mesh):
    n_dev = mesh.shape['cp']
    forward_perm = [(i, (i + 1) % n_dev) for i in range(n_dev)]
    row_spec = P(('dp', 'cp'))

    def local_fn(q_tok, k_tok, v_tok, fwd_out, d_out, lse_row):
        softmax_scale = q_tok.shape[-1] ** -0.5
        my_index = lax.axis_index('cp')
        row_delta = jnp.einsum('rgd,rgd->rg', d_out, fwd_out, preferred_element_type=jnp.float32)

        def accumulate(step, state):
            def pair_update(state_in):
                dq_acc, k_cur, v_cur, dk_acc, dv_acc = state_in
                prob_low, score_low = pair_scores(q_tok, d_out, lse_row, row_delta, k_cur, v_cur, step == 0, softmax_scale)
                dq_acc = dq_acc + jnp.einsum('rgc,cd->rgd', score_low, k_cur, preferred_element_type=jnp.float32)
                dk_acc = dk_acc + jnp.einsum('rgc,rgd->cd', score_low, q_tok, preferred_element_type=jnp.float32)
                dv_acc = dv_acc + jnp.einsum('rgc,rgd->cd', prob_low, d_out, preferred_element_type=jnp.float32)
                return (dq_acc, k_cur, v_cur, dk_acc, dv_acc)

            def keep_state(state_in):
                return state_in

            return lax.cond(step <= my_index, pair_update, keep_state, state)

        def step_fn(step, state):
            dq_acc, k_cur, v_cur, dk_acc, dv_acc = accumulate(step, state)
            k_next = lax.ppermute(k_cur, 'cp', forward_perm)
            v_next = lax.ppermute(v_cur, 'cp', forward_perm)
            dk_next = lax.ppermute(dk_acc, 'cp', forward_perm)
            dv_next = lax.ppermute(dv_acc, 'cp', forward_perm)
            return (dq_acc, k_next, v_next, dk_next, dv_next)

        kv_zeros = jnp.zeros(k_tok.shape, jnp.float32)
        state = (jnp.zeros(q_tok.shape, jnp.float32), k_tok, v_tok, kv_zeros, kv_zeros)
        state = lax.fori_loop(0, n_dev - 1, step_fn, state)
        dq_acc, k_cur, v_cur, dk_acc, dv_acc = accumulate(n_dev - 1, state)
        dk_home = lax.ppermute(dk_acc, 'cp', forward_perm)
        dv_home = lax.ppermute(dv_acc, 'cp', forward_perm)
        grad_q = (dq_acc * softmax_scale).astype(jnp.bfloat16)
        grad_k = (dk_home * softmax_scale).astype(jnp.bfloat16)
        grad_v = dv_home.astype(jnp.bfloat16)
        return grad_q, grad_k, grad_v

    return jax.shard_map(local_fn, mesh=mesh, in_specs=(row_spec, row_spec, row_spec, row_spec, row_spec, row_spec), out_specs=(row_spec, row_spec, row_spec), check_vma=False)
```

profile of v0, /device:TPU:112, one launch (start us, length us, event | category | flops | bytes accessed | tf_op | source)
XLA Modules:
  0.0 286.5 jit_solution(7337619581036160361)
XLA Ops:
  6.1 252.1 %while.21 = (s32[]{:T(128)}, f32[1024,3,128]{2,0,1:T(8,128)S(1)}, bf16[1024,128]{1,0:T(8,128)(2,1)S(1)}, bf16[1024,128]{1,0:T(8,128)(2,1)}, f32[1024,128]{1,0:T(...) while((s32[]{:T(128)}, f32[1024,3,128]{2,0,1:T(8,128)S(1)}, ...), condition=%wide.region_3.4_spmd, body=%wide.region_0.3_spmd.sunk | while | flops 4060741632 | bytes 84759048 | solution.py:51
  7.1 17.0 %conditional.4 = ((f32[1024,3,128]{2,0,1:T(8,128)S(1)}, f32[1024,128]{1,0:T(8,128)S(1)}, f32[1024,128]{1,0:T(8,128)})) conditional(s32[]{:T(128)} %convert_element_type.52, (f32[1024,3,128]{2,0,1:T(8,128)S(1)}, f32[1024,128]{1,0:T(8,128)S(1)}, f32[1024,128]{1,0:T(8,128)}) %tuple.50, (s32[]{:T(128)}, bf16[1024,3,128]{2,0,1:T(8,128)(2,1)}, ...), branch_computations={%region_1.0_spmd, %region_2.2_spmd} | conditional | flops 4060741632 | bytes 75321472 | solution.py:39
  7.5 3.0 %fusion.14 = f32[1024,3,1024]{2,0,1:T(8,128)S(1)} fusion(bf16[1024,3,128]{2,0,1:T(8,128)(2,1)} %get-tuple-element.225, bf16[1024,128]{1,0:T(8,128)(2,1)S(1)} %get-tuple-element.226), kind=kOutput, calls=%fused_computation.14 | convolution fusion | flops 805306368 | bytes 13631488 | tf_op jit(solution)/shard_map/while/body/eval_jaxpr/cond/branch_1_fun/rgd,cd->rgc/dot_general | solution.py:8
  10.5 5.5 %fusion.8 = f32[1024,128]{1,0:T(8,128)} fusion(f32[1024,128]{1,0:T(8,128)} %get-tuple-element.232, bf16[1024,3,128]{2,0,1:T(8,128)(2,1)S(1)} %copy-done.2, f32[1024,3,1024]{2,0,1:T(8,128)S(1)} %fusion.14, f32[1024,3]{0,1:T(4,128)S(1)} %copy-done.4, pred[1024,1024]{1,0:T(8,128)(4,1)S(1)} %fusion.4), kind=kOutput, calls=%fused_computation.10 | convolution fusion | flops 818020352 | bytes 15478784 | tf_op jit(solution)/shard_map/while/body/eval_jaxpr/cond/branch_1_fun/rgc,rgd->cd/dot_general | solution.py:33
  16.0 4.3 %multiply_convert_fusion = bf16[1024,3,1024]{2,0,1:T(8,128)(2,1)S(1)} fusion(f32[1024,3,1024]{2,0,1:T(8,128)S(1)} %fusion.14, f32[1024,3]{0,1:T(4,128)S(1)} %get-tuple-element.230, f32[1024,3]{0,1:T(4,128)S(1)} %copy-done.4, pred[1024,1024]{1,0:T(8,128)(4,1)S(1)} %fusion.4, bf16[1024,3,128]{2,0,1:T(8,128)(2,1)S(1)} %copy-done.2, ...), kind=kOutput, calls=%fused_computation | convolution fusion | flops 824180736 | bytes 20996096 | tf_op jit(solution)/shard_map/while/body/eval_jaxpr/cond/branch_1_fun/rgd,cd->rgc/dot_general | solution.py:12
  28.4 6.1 %collective-permute-done.2 = f32[1024,128]{1,0:T(8,128)} collective-permute-done((f32[1024,128]{1,0:T(8,128)S(1)}, f32[1024,128]{1,0:T(8,128)}, u32[]{:S(2)}, u32[]{:S(2)}) %collective-permute-start.2) | collective-permute-done | bytes 524320 | tf_op jit(solution)/shard_map/while/body/eval_jaxpr/ppermute | solution.py:45
  35.5 4.6 %collective-permute-done.3 = f32[1024,128]{1,0:T(8,128)S(1)} collective-permute-done((f32[1024,128]{1,0:T(8,128)}, f32[1024,128]{1,0:T(8,128)S(1)}, u32[]{:S(2)}, u32[]{:S(2)}) %collective-permute-start.3) | collective-permute-done | bytes 524320 | tf_op jit(solution)/shard_map/while/body/eval_jaxpr/ppermute | solution.py:46
  46.7 15.4 %collective-permute-start.2 = (f32[1024,128]{1,0:T(8,128)S(1)}, f32[1024,128]{1,0:T(8,128)}, u32[]{:S(2)}, u32[]{:S(2)}) collective-permute-start(f32[1024,128]{1,0:T(8,128)S(1)} %get-tuple-element.369), channel_id=1, source_target_pairs={{0,1},{1,2},{2,3},{3,4},{4,5},{5,6},{6,7},{7,0},{8,9},{9,10},{10,1... | collective-permute-start | bytes 1572872 | tf_op jit(solution)/shard_map/while/body/eval_jaxpr/ppermute | solution.py:45
  66.3 3.6 %collective-permute-done.2 = f32[1024,128]{1,0:T(8,128)} collective-permute-done((f32[1024,128]{1,0:T(8,128)S(1)}, f32[1024,128]{1,0:T(8,128)}, u32[]{:S(2)}, u32[]{:S(2)}) %collective-permute-start.2) | collective-permute-done | bytes 524320 | tf_op jit(solution)/shard_map/while/body/eval_jaxpr/ppermute | solution.py:45
  70.9 4.6 %collective-permute-done.3 = f32[1024,128]{1,0:T(8,128)S(1)} collective-permute-done((f32[1024,128]{1,0:T(8,128)}, f32[1024,128]{1,0:T(8,128)S(1)}, u32[]{:S(2)}, u32[]{:S(2)}) %collective-permute-start.3) | collective-permute-done | bytes 524320 | tf_op jit(solution)/shard_map/while/body/eval_jaxpr/ppermute | solution.py:46
  82.9 19.5 %collective-permute-start.3 = (f32[1024,128]{1,0:T(8,128)}, f32[1024,128]{1,0:T(8,128)S(1)}, u32[]{:S(2)}, u32[]{:S(2)}) collective-permute-start(f32[1024,128]{1,0:T(8,128)} %get-tuple-element.370), channel_id=1, source_target_pairs={{0,1},{1,2},{2,3},{3,4},{4,5},{5,6},{6,7},{7,0},{8,9},{9,10},{10,1... | collective-permute-start | bytes 1572872 | tf_op jit(solution)/shard_map/while/body/eval_jaxpr/ppermute | solution.py:46
  106.3 4.6 %collective-permute-done.3 = f32[1024,128]{1,0:T(8,128)S(1)} collective-permute-done((f32[1024,128]{1,0:T(8,128)}, f32[1024,128]{1,0:T(8,128)S(1)}, u32[]{:S(2)}, u32[]{:S(2)}) %collective-permute-start.3) | collective-permute-done | bytes 524320 | tf_op jit(solution)/shard_map/while/body/eval_jaxpr/ppermute | solution.py:46
  117.5 3.3 %collective-permute-start.2 = (f32[1024,128]{1,0:T(8,128)S(1)}, f32[1024,128]{1,0:T(8,128)}, u32[]{:S(2)}, u32[]{:S(2)}) collective-permute-start(f32[1024,128]{1,0:T(8,128)S(1)} %get-tuple-element.369), channel_id=1, source_target_pairs={{0,1},{1,2},{2,3},{3,4},{4,5},{5,6},{6,7},{7,0},{8,9},{9,10},{10,1... | collective-permute-start | bytes 1572872 | tf_op jit(solution)/shard_map/while/body/eval_jaxpr/ppermute | solution.py:45
  123.4 16.2 %collective-permute-start = (bf16[1024,128]{1,0:T(8,128)(2,1)S(1)}, bf16[1024,128]{1,0:T(8,128)(2,1)S(1)}, u32[]{:S(2)}, u32[]{:S(2)}) collective-permute-start(bf16[1024,128]{1,0:T(8,128)(2,1)S(1)} %copy.36), channel_id=1, source_target_pairs={{0,1},{1,2},{2,3},{3,4},{4,5},{5,6},{6,7},{7,0},{8,9},{9,10},{10,1... | collective-permute-start | bytes 786440 | tf_op jit(solution)/shard_map/while/body/eval_jaxpr/ppermute | solution.py:43
  143.2 3.2 %collective-permute-done.3 = f32[1024,128]{1,0:T(8,128)S(1)} collective-permute-done((f32[1024,128]{1,0:T(8,128)}, f32[1024,128]{1,0:T(8,128)S(1)}, u32[]{:S(2)}, u32[]{:S(2)}) %collective-permute-start.3) | collective-permute-done | bytes 524320 | tf_op jit(solution)/shard_map/while/body/eval_jaxpr/ppermute | solution.py:46
  154.9 5.6 %collective-permute-start = (bf16[1024,128]{1,0:T(8,128)(2,1)S(1)}, bf16[1024,128]{1,0:T(8,128)(2,1)S(1)}, u32[]{:S(2)}, u32[]{:S(2)}) collective-permute-start(bf16[1024,128]{1,0:T(8,128)(2,1)S(1)} %copy.36), channel_id=1, source_target_pairs={{0,1},{1,2},{2,3},{3,4},{4,5},{5,6},{6,7},{7,0},{8,9},{9,10},{10,1... | collective-permute-start | bytes 786440 | tf_op jit(solution)/shard_map/while/body/eval_jaxpr/ppermute | solution.py:43
  160.5 19.5 %collective-permute-start.1 = (bf16[1024,128]{1,0:T(8,128)(2,1)S(1)}, bf16[1024,128]{1,0:T(8,128)(2,1)}, u32[]{:S(2)}, u32[]{:S(2)}) collective-permute-start(bf16[1024,128]{1,0:T(8,128)(2,1)S(1)} %copy.37), channel_id=1, source_target_pairs={{0,1},{1,2},{2,3},{3,4},{4,5},{5,6},{6,7},{7,0},{8,9},{9,10},{10,1... | collective-permute-start | bytes 786440 | tf_op jit(solution)/shard_map/while/body/eval_jaxpr/ppermute | solution.py:44
  189.7 8.7 %collective-permute-start = (bf16[1024,128]{1,0:T(8,128)(2,1)S(1)}, bf16[1024,128]{1,0:T(8,128)(2,1)S(1)}, u32[]{:S(2)}, u32[]{:S(2)}) collective-permute-start(bf16[1024,128]{1,0:T(8,128)(2,1)S(1)} %copy.36), channel_id=1, source_target_pairs={{0,1},{1,2},{2,3},{3,4},{4,5},{5,6},{6,7},{7,0},{8,9},{9,10},{10,1... | collective-permute-start | bytes 786440 | tf_op jit(solution)/shard_map/while/body/eval_jaxpr/ppermute | solution.py:43
  200.9 10.6 %collective-permute-done.2 = f32[1024,128]{1,0:T(8,128)} collective-permute-done((f32[1024,128]{1,0:T(8,128)S(1)}, f32[1024,128]{1,0:T(8,128)}, u32[]{:S(2)}, u32[]{:S(2)}) %collective-permute-start.2) | collective-permute-done | bytes 524320 | tf_op jit(solution)/shard_map/while/body/eval_jaxpr/ppermute | solution.py:45
  212.6 4.6 %collective-permute-done.3 = f32[1024,128]{1,0:T(8,128)S(1)} collective-permute-done((f32[1024,128]{1,0:T(8,128)}, f32[1024,128]{1,0:T(8,128)S(1)}, u32[]{:S(2)}, u32[]{:S(2)}) %collective-permute-start.3) | collective-permute-done | bytes 524320 | tf_op jit(solution)/shard_map/while/body/eval_jaxpr/ppermute | solution.py:46
  223.9 5.7 %collective-permute-start = (bf16[1024,128]{1,0:T(8,128)(2,1)S(1)}, bf16[1024,128]{1,0:T(8,128)(2,1)S(1)}, u32[]{:S(2)}, u32[]{:S(2)}) collective-permute-start(bf16[1024,128]{1,0:T(8,128)(2,1)S(1)} %copy.36), channel_id=1, source_target_pairs={{0,1},{1,2},{2,3},{3,4},{4,5},{5,6},{6,7},{7,0},{8,9},{9,10},{10,1... | collective-permute-start | bytes 786440 | tf_op jit(solution)/shard_map/while/body/eval_jaxpr/ppermute | solution.py:43
  232.1 14.8 %collective-permute-done.2 = f32[1024,128]{1,0:T(8,128)} collective-permute-done((f32[1024,128]{1,0:T(8,128)S(1)}, f32[1024,128]{1,0:T(8,128)}, u32[]{:S(2)}, u32[]{:S(2)}) %collective-permute-start.2) | collective-permute-done | bytes 524320 | tf_op jit(solution)/shard_map/while/body/eval_jaxpr/ppermute | solution.py:45
  248.0 4.6 %collective-permute-done.3 = f32[1024,128]{1,0:T(8,128)S(1)} collective-permute-done((f32[1024,128]{1,0:T(8,128)}, f32[1024,128]{1,0:T(8,128)S(1)}, u32[]{:S(2)}, u32[]{:S(2)}) %collective-permute-start.3) | collective-permute-done | bytes 524320 | tf_op jit(solution)/shard_map/while/body/eval_jaxpr/ppermute | solution.py:46
  261.4 23.7 %collective-permute-done.5 = bf16[1024,128]{1,0:T(8,128)(2,1)S(1)} collective-permute-done((bf16[1024,128]{1,0:T(8,128)(2,1)S(1)}, bf16[1024,128]{1,0:T(8,128)(2,1)S(1)}, u32[]{:S(2)}, u32[]{:S(2)}) %collective-permute-start.5) | collective-permute-done | bytes 262176 | tf_op jit(solution)/shard_map/ppermute | solution.py:54
  (95 shorter events, 93.8 us)
Async XLA Ops:
  24.2 15.9 %collective-permute-start.3 = (f32[1024,128]{1,0:T(8,128)}, f32[1024,128]{1,0:T(8,128)S(1)}, u32[]{:S(2)}, u32[]{:S(2)}) collective-permute-start(f32[1024,128]{1,0:T(8,128)} %get-tuple-element.370), channel_id=1, source_target_pairs={{0,1},{1,2},{2,3},{3,4},{4,5},{5,6},{6,7},{7,0},{8,9},{9,10},{10,1... | collective-permute-start | bytes 1572872 | tf_op jit(solution)/shard_map/while/body/eval_jaxpr/ppermute | solution.py:46
  26.6 16.2 %collective-permute-start = (bf16[1024,128]{1,0:T(8,128)(2,1)S(1)}, bf16[1024,128]{1,0:T(8,128)(2,1)S(1)}, u32[]{:S(2)}, u32[]{:S(2)}) collective-permute-start(bf16[1024,128]{1,0:T(8,128)(2,1)S(1)} %copy.36), channel_id=1, source_target_pairs={{0,1},{1,2},{2,3},{3,4},{4,5},{5,6},{6,7},{7,0},{8,9},{9,10},{10,1... | collective-permute-start | bytes 786440 | tf_op jit(solution)/shard_map/while/body/eval_jaxpr/ppermute | solution.py:43
  26.7 19.0 %collective-permute-start.1 = (bf16[1024,128]{1,0:T(8,128)(2,1)S(1)}, bf16[1024,128]{1,0:T(8,128)(2,1)}, u32[]{:S(2)}, u32[]{:S(2)}) collective-permute-start(bf16[1024,128]{1,0:T(8,128)(2,1)S(1)} %copy.37), channel_id=1, source_target_pairs={{0,1},{1,2},{2,3},{3,4},{4,5},{5,6},{6,7},{7,0},{8,9},{9,10},{10,1... | collective-permute-start | bytes 786440 | tf_op jit(solution)/shard_map/while/body/eval_jaxpr/ppermute | solution.py:44
  46.7 23.2 %collective-permute-start.2 = (f32[1024,128]{1,0:T(8,128)S(1)}, f32[1024,128]{1,0:T(8,128)}, u32[]{:S(2)}, u32[]{:S(2)}) collective-permute-start(f32[1024,128]{1,0:T(8,128)S(1)} %get-tuple-element.369), channel_id=1, source_target_pairs={{0,1},{1,2},{2,3},{3,4},{4,5},{5,6},{6,7},{7,0},{8,9},{9,10},{10,1... | collective-permute-start | bytes 1572872 | tf_op jit(solution)/shard_map/while/body/eval_jaxpr/ppermute | solution.py:45
  64.6 16.5 %collective-permute-start.1 = (bf16[1024,128]{1,0:T(8,128)(2,1)S(1)}, bf16[1024,128]{1,0:T(8,128)(2,1)}, u32[]{:S(2)}, u32[]{:S(2)}) collective-permute-start(bf16[1024,128]{1,0:T(8,128)(2,1)S(1)} %copy.37), channel_id=1, source_target_pairs={{0,1},{1,2},{2,3},{3,4},{4,5},{5,6},{6,7},{7,0},{8,9},{9,10},{10,1... | collective-permute-start | bytes 786440 | tf_op jit(solution)/shard_map/while/body/eval_jaxpr/ppermute | solution.py:44
  82.1 23.2 %collective-permute-start.2 = (f32[1024,128]{1,0:T(8,128)S(1)}, f32[1024,128]{1,0:T(8,128)}, u32[]{:S(2)}, u32[]{:S(2)}) collective-permute-start(f32[1024,128]{1,0:T(8,128)S(1)} %get-tuple-element.369), channel_id=1, source_target_pairs={{0,1},{1,2},{2,3},{3,4},{4,5},{5,6},{6,7},{7,0},{8,9},{9,10},{10,1... | collective-permute-start | bytes 1572872 | tf_op jit(solution)/shard_map/while/body/eval_jaxpr/ppermute | solution.py:45
  82.9 28.0 %collective-permute-start.3 = (f32[1024,128]{1,0:T(8,128)}, f32[1024,128]{1,0:T(8,128)S(1)}, u32[]{:S(2)}, u32[]{:S(2)}) collective-permute-start(f32[1024,128]{1,0:T(8,128)} %get-tuple-element.370), channel_id=1, source_target_pairs={{0,1},{1,2},{2,3},{3,4},{4,5},{5,6},{6,7},{7,0},{8,9},{9,10},{10,1... | collective-permute-start | bytes 1572872 | tf_op jit(solution)/shard_map/while/body/eval_jaxpr/ppermute | solution.py:46
  117.5 24.6 %collective-permute-start.2 = (f32[1024,128]{1,0:T(8,128)S(1)}, f32[1024,128]{1,0:T(8,128)}, u32[]{:S(2)}, u32[]{:S(2)}) collective-permute-start(f32[1024,128]{1,0:T(8,128)S(1)} %get-tuple-element.369), channel_id=1, source_target_pairs={{0,1},{1,2},{2,3},{3,4},{4,5},{5,6},{6,7},{7,0},{8,9},{9,10},{10,1... | collective-permute-start | bytes 1572872 | tf_op jit(solution)/shard_map/while/body/eval_jaxpr/ppermute | solution.py:45
  120.9 25.5 %collective-permute-start.3 = (f32[1024,128]{1,0:T(8,128)}, f32[1024,128]{1,0:T(8,128)S(1)}, u32[]{:S(2)}, u32[]{:S(2)}) collective-permute-start(f32[1024,128]{1,0:T(8,128)} %get-tuple-element.370), channel_id=1, source_target_pairs={{0,1},{1,2},{2,3},{3,4},{4,5},{5,6},{6,7},{7,0},{8,9},{9,10},{10,1... | collective-permute-start | bytes 1572872 | tf_op jit(solution)/shard_map/while/body/eval_jaxpr/ppermute | solution.py:46
  123.4 25.8 %collective-permute-start = (bf16[1024,128]{1,0:T(8,128)(2,1)S(1)}, bf16[1024,128]{1,0:T(8,128)(2,1)S(1)}, u32[]{:S(2)}, u32[]{:S(2)}) collective-permute-start(bf16[1024,128]{1,0:T(8,128)(2,1)S(1)} %copy.36), channel_id=1, source_target_pairs={{0,1},{1,2},{2,3},{3,4},{4,5},{5,6},{6,7},{7,0},{8,9},{9,10},{10,1... | collective-permute-start | bytes 786440 | tf_op jit(solution)/shard_map/while/body/eval_jaxpr/ppermute | solution.py:43
  152.9 27.1 %collective-permute-start.2 = (f32[1024,128]{1,0:T(8,128)S(1)}, f32[1024,128]{1,0:T(8,128)}, u32[]{:S(2)}, u32[]{:S(2)}) collective-permute-start(f32[1024,128]{1,0:T(8,128)S(1)} %get-tuple-element.369), channel_id=1, source_target_pairs={{0,1},{1,2},{2,3},{3,4},{4,5},{5,6},{6,7},{7,0},{8,9},{9,10},{10,1... | collective-permute-start | bytes 1572872 | tf_op jit(solution)/shard_map/while/body/eval_jaxpr/ppermute | solution.py:45
  153.0 28.7 %collective-permute-start.3 = (f32[1024,128]{1,0:T(8,128)}, f32[1024,128]{1,0:T(8,128)S(1)}, u32[]{:S(2)}, u32[]{:S(2)}) collective-permute-start(f32[1024,128]{1,0:T(8,128)} %get-tuple-element.370), channel_id=1, source_target_pairs={{0,1},{1,2},{2,3},{3,4},{4,5},{5,6},{6,7},{7,0},{8,9},{9,10},{10,1... | collective-permute-start | bytes 1572872 | tf_op jit(solution)/shard_map/while/body/eval_jaxpr/ppermute | solution.py:46
  154.9 29.7 %collective-permute-start = (bf16[1024,128]{1,0:T(8,128)(2,1)S(1)}, bf16[1024,128]{1,0:T(8,128)(2,1)S(1)}, u32[]{:S(2)}, u32[]{:S(2)}) collective-permute-start(bf16[1024,128]{1,0:T(8,128)(2,1)S(1)} %copy.36), channel_id=1, source_target_pairs={{0,1},{1,2},{2,3},{3,4},{4,5},{5,6},{6,7},{7,0},{8,9},{9,10},{10,1... | collective-permute-start | bytes 786440 | tf_op jit(solution)/shard_map/while/body/eval_jaxpr/ppermute | solution.py:43
  160.5 26.9 %collective-permute-start.1 = (bf16[1024,128]{1,0:T(8,128)(2,1)S(1)}, bf16[1024,128]{1,0:T(8,128)(2,1)}, u32[]{:S(2)}, u32[]{:S(2)}) collective-permute-start(bf16[1024,128]{1,0:T(8,128)(2,1)S(1)} %copy.37), channel_id=1, source_target_pairs={{0,1},{1,2},{2,3},{3,4},{4,5},{5,6},{6,7},{7,0},{8,9},{9,10},{10,1... | collective-permute-start | bytes 786440 | tf_op jit(solution)/shard_map/while/body/eval_jaxpr/ppermute | solution.py:44
  188.4 23.2 %collective-permute-start.2 = (f32[1024,128]{1,0:T(8,128)S(1)}, f32[1024,128]{1,0:T(8,128)}, u32[]{:S(2)}, u32[]{:S(2)}) collective-permute-start(f32[1024,128]{1,0:T(8,128)S(1)} %get-tuple-element.369), channel_id=1, source_target_pairs={{0,1},{1,2},{2,3},{3,4},{4,5},{5,6},{6,7},{7,0},{8,9},{9,10},{10,1... | collective-permute-start | bytes 1572872 | tf_op jit(solution)/shard_map/while/body/eval_jaxpr/ppermute | solution.py:45
  188.4 28.7 %collective-permute-start.3 = (f32[1024,128]{1,0:T(8,128)}, f32[1024,128]{1,0:T(8,128)S(1)}, u32[]{:S(2)}, u32[]{:S(2)}) collective-permute-start(f32[1024,128]{1,0:T(8,128)} %get-tuple-element.370), channel_id=1, source_target_pairs={{0,1},{1,2},{2,3},{3,4},{4,5},{5,6},{6,7},{7,0},{8,9},{9,10},{10,1... | collective-permute-start | bytes 1572872 | tf_op jit(solution)/shard_map/while/body/eval_jaxpr/ppermute | solution.py:46
  189.7 30.3 %collective-permute-start = (bf16[1024,128]{1,0:T(8,128)(2,1)S(1)}, bf16[1024,128]{1,0:T(8,128)(2,1)S(1)}, u32[]{:S(2)}, u32[]{:S(2)}) collective-permute-start(bf16[1024,128]{1,0:T(8,128)(2,1)S(1)} %copy.36), channel_id=1, source_target_pairs={{0,1},{1,2},{2,3},{3,4},{4,5},{5,6},{6,7},{7,0},{8,9},{9,10},{10,1... | collective-permute-start | bytes 786440 | tf_op jit(solution)/shard_map/while/body/eval_jaxpr/ppermute | solution.py:43
  198.4 24.4 %collective-permute-start.1 = (bf16[1024,128]{1,0:T(8,128)(2,1)S(1)}, bf16[1024,128]{1,0:T(8,128)(2,1)}, u32[]{:S(2)}, u32[]{:S(2)}) collective-permute-start(bf16[1024,128]{1,0:T(8,128)(2,1)S(1)} %copy.37), channel_id=1, source_target_pairs={{0,1},{1,2},{2,3},{3,4},{4,5},{5,6},{6,7},{7,0},{8,9},{9,10},{10,1... | collective-permute-start | bytes 786440 | tf_op jit(solution)/shard_map/while/body/eval_jaxpr/ppermute | solution.py:44
  223.8 23.2 %collective-permute-start.2 = (f32[1024,128]{1,0:T(8,128)S(1)}, f32[1024,128]{1,0:T(8,128)}, u32[]{:S(2)}, u32[]{:S(2)}) collective-permute-start(f32[1024,128]{1,0:T(8,128)S(1)} %get-tuple-element.369), channel_id=1, source_target_pairs={{0,1},{1,2},{2,3},{3,4},{4,5},{5,6},{6,7},{7,0},{8,9},{9,10},{10,1... | collective-permute-start | bytes 1572872 | tf_op jit(solution)/shard_map/while/body/eval_jaxpr/ppermute | solution.py:45
  223.9 28.7 %collective-permute-start.3 = (f32[1024,128]{1,0:T(8,128)}, f32[1024,128]{1,0:T(8,128)S(1)}, u32[]{:S(2)}, u32[]{:S(2)}) collective-permute-start(f32[1024,128]{1,0:T(8,128)} %get-tuple-element.370), channel_id=1, source_target_pairs={{0,1},{1,2},{2,3},{3,4},{4,5},{5,6},{6,7},{7,0},{8,9},{9,10},{10,1... | collective-permute-start | bytes 1572872 | tf_op jit(solution)/shard_map/while/body/eval_jaxpr/ppermute | solution.py:46
  223.9 31.5 %collective-permute-start = (bf16[1024,128]{1,0:T(8,128)(2,1)S(1)}, bf16[1024,128]{1,0:T(8,128)(2,1)S(1)}, u32[]{:S(2)}, u32[]{:S(2)}) collective-permute-start(bf16[1024,128]{1,0:T(8,128)(2,1)S(1)} %copy.36), channel_id=1, source_target_pairs={{0,1},{1,2},{2,3},{3,4},{4,5},{5,6},{6,7},{7,0},{8,9},{9,10},{10,1... | collective-permute-start | bytes 786440 | tf_op jit(solution)/shard_map/while/body/eval_jaxpr/ppermute | solution.py:43
  229.6 28.6 %collective-permute-start.1 = (bf16[1024,128]{1,0:T(8,128)(2,1)S(1)}, bf16[1024,128]{1,0:T(8,128)(2,1)}, u32[]{:S(2)}, u32[]{:S(2)}) collective-permute-start(bf16[1024,128]{1,0:T(8,128)(2,1)S(1)} %copy.37), channel_id=1, source_target_pairs={{0,1},{1,2},{2,3},{3,4},{4,5},{5,6},{6,7},{7,0},{8,9},{9,10},{10,1... | collective-permute-start | bytes 786440 | tf_op jit(solution)/shard_map/while/body/eval_jaxpr/ppermute | solution.py:44
  258.2 26.9 %collective-permute-start.4 = (f32[1024,128]{1,0:T(8,128)S(1)}, f32[1024,128]{1,0:T(8,128)S(1)}, u32[]{:S(2)}, u32[]{:S(2)}) collective-permute-start(f32[1024,128]{1,0:T(8,128)S(1)} %get-tuple-element.274), channel_id=1, source_target_pairs={{0,1},{1,2},{2,3},{3,4},{4,5},{5,6},{6,7},{7,0},{8,9},{9,10},{10,1... | collective-permute-start | bytes 1572872 | tf_op jit(solution)/shard_map/ppermute | solution.py:53
  259.3 25.8 %collective-permute-start.5 = (bf16[1024,128]{1,0:T(8,128)(2,1)S(1)}, bf16[1024,128]{1,0:T(8,128)(2,1)S(1)}, u32[]{:S(2)}, u32[]{:S(2)}) collective-permute-start(bf16[1024,128]{1,0:T(8,128)(2,1)S(1)} %convert.12), channel_id=1, source_target_pairs={{0,1},{1,2},{2,3},{3,4},{4,5},{5,6},{6,7},{7,0},{8,9},{9,10},{10,1... | collective-permute-start | bytes 786440 | tf_op jit(solution)/shard_map/ppermute | solution.py:54
  (9 other events, 85.5 us)
where the time goes:
time: 288 us; the launch traced here: 287 us
  waiting for transfers between devices  120 us (42%)
  starting transfers between devices  119 us (41%)
  local copies, waits for them, and re-layouts  23.9 us (8%)
  matrix products  16.6 us (6%)
  other arithmetic  5.05 us (2%)
    ppermute x7, starting transfers between devices, step_fn(): k_next = lax.ppermute(k_cur, 'cp', forward_perm)  36.5 us
    ppermute x7, waiting for transfers between devices, step_fn(): dk_next = lax.ppermute(dk_acc, 'cp', forward_perm)  36.3 us
    ppermute x7, starting transfers between devices, step_fn(): v_next = lax.ppermute(v_cur, 'cp', forward_perm)  32 us
    ppermute x7, starting transfers between devices, step_fn(): dv_next = lax.ppermute(dv_acc, 'cp', forward_perm)  30.1 us
    ppermute x7, waiting for transfers between devices, step_fn(): dv_next = lax.ppermute(dv_acc, 'cp', forward_perm)  26.7 us
    ppermute x1, waiting for transfers between devices, local_fn(): dv_home = lax.ppermute(dv_acc, 'cp', forward_perm)  23.7 us
    ppermute x7, starting transfers between devices, step_fn(): dk_next = lax.ppermute(dk_acc, 'cp', forward_perm)  19.8 us
    ppermute x7, waiting for transfers between devices, step_fn(): v_next = lax.ppermute(v_cur, 'cp', forward_perm)  19.7 us
  transfers between devices with their start and end apart: 30, of which 27 were waited for; matrix products, arithmetic and copies ran while one was open for 5% of the time, Pallas kernels for 0%

commit v1 on v0

v1 whole, which is shorter than its diff:
```python
import functools
import math

import jax
import jax.numpy as jnp
from jax import lax
from jax.experimental import pallas as pl
from jax.experimental.pallas import tpu as pltpu
from jax.sharding import PartitionSpec as P

NT = (((1,), (1,)), ((), ()))
NN = (((1,), (0,)), ((), ()))
LOG2E = math.log2(math.e)
A, B, R = 0, 1, 2


def dot(a, b, dims):
    return lax.dot_general(a, b, dims, preferred_element_type=jnp.float32)


def kernel(n_dev, q_hbm, do_hbm, ld_hbm, k_hbm, v_hbm, gq, gk, gv,
           q, do, qt, dot_t, ld, lseb, delb, kv, acc, dq, rbuf, rhalf, rdq,
           in_sem, pair_send, pair_recv, kv_send, kv_recv, g_send, g_recv, f_send, d_send, d_recv):
    heads, rows, dim = q.shape[1:]
    half = rows // 2
    scale = dim ** -0.5
    scale2 = scale * LOG2E
    own_slot = n_dev // 2
    n_chip = n_dev // 2

    me = lax.axis_index('cp')
    chip, core = me // 2, me % 2
    other = 1 - core
    partner = chip * 2 + other

    def at(chip_id):
        return {'cp': chip_id * 2 + core}

    loads = [
        pltpu.make_async_copy(k_hbm, kv.at[own_slot + core, 0], in_sem.at[0]),
        pltpu.make_async_copy(v_hbm, kv.at[own_slot + core, 1], in_sem.at[1]),
        pltpu.make_async_copy(q_hbm, q.at[core], in_sem.at[2]),
        pltpu.make_async_copy(do_hbm, do.at[core], in_sem.at[3]),
        pltpu.make_async_copy(ld_hbm, ld.at[core], in_sem.at[4]),
    ]
    for copy in loads:
        copy.start()

    barrier = pltpu.get_barrier_semaphore()
    for d in range(1, n_dev):
        pl.semaphore_signal(barrier, inc=1, device_id={'cp': lax.rem(me + d, n_dev)}, device_id_type=pl.DeviceIdType.MESH)
    acc[...] = jnp.zeros_like(acc)
    dq[...] = jnp.zeros_like(dq)
    pl.semaphore_wait(barrier, n_dev - 1)

    def remote(src, dst, send, recv, device):
        return pltpu.make_async_remote_copy(src_ref=src, dst_ref=dst, send_sem=send, recv_sem=recv,
                                            device_id=device, device_id_type=pl.DeviceIdType.MESH)

    def kv_copies(slot, src_slot, sem_row, device):
        return [remote(kv.at[src_slot, i], kv.at[slot, i], kv_send.at[sem_row, i], kv_recv.at[slot, i], device)
                for i in range(2)]

    def kv_send_own(sem_row, to_chip):
        for copy in kv_copies(chip, own_slot + core, sem_row, at(to_chip)):
            copy.start()

    def kv_wait_sent(sem_row):
        for copy in kv_copies(0, 0, sem_row, at(chip)):
            copy.wait_send()

    last = n_chip - 1
    late_next = jnp.logical_and(chip == last - 1, core == 0)
    late_wrap = jnp.logical_and(chip == 0, core == 1)
    loads[0].wait()
    loads[1].wait()

    @pl.when(jnp.logical_and(chip < last, jnp.logical_not(late_next)))
    def _():
        kv_send_own(0, chip + 1)

    @pl.when(jnp.logical_and(chip == 0, core == 0))
    def _():
        kv_send_own(1, last)

    pair = [
        remote(kv.at[own_slot + core, 0], kv.at[own_slot + core, 0], pair_send.at[0], pair_recv.at[0], {'cp': partner}),
        remote(kv.at[own_slot + core, 1], kv.at[own_slot + core, 1], pair_send.at[1], pair_recv.at[1], {'cp': partner}),
        remote(q.at[core], q.at[core], pair_send.at[2], pair_recv.at[2], {'cp': partner}),
        remote(do.at[core], do.at[core], pair_send.at[3], pair_recv.at[3], {'cp': partner}),
        remote(ld.at[core], ld.at[core], pair_send.at[4], pair_recv.at[4], {'cp': partner}),
    ]
    for i in (2, 3, 4):
        loads[i].wait()
        pair[i].start()
    pair[0].start()
    pair[1].start()

    def prep(b):
        qt[b] = q[b].reshape(heads * rows, dim).T
        dot_t[b] = do[b].reshape(heads * rows, dim).T
        for g in range(heads):
            lseb[b, g] = jnp.broadcast_to(ld[b, :, g:g + 1], (rows, dim))
            delb[b, g] = jnp.broadcast_to(ld[b, :, heads + g:heads + g + 1], (rows, dim))

    def tile(b, row_half, slot, h, masked):
        size = rows if row_half is None else half
        first = 0 if row_half is None else row_half * half
        start = pl.multiple_of(h * half, half)
        kk = kv[slot, 0, pl.ds(start, half), :]
        vv = kv[slot, 1, pl.ds(start, half), :]
        part = lambda ref: ref[b, :, first:first + size, :].reshape(heads * size, dim)
        part_t = lambda ref: jnp.concatenate(
            [ref[b, :, g * rows + first:g * rows + first + size] for g in range(heads)], axis=1)
        wide = lambda x: jnp.concatenate([x] * (half // dim), axis=1)
        logits = dot(part(q), kk, NT)
        prob = jnp.exp2(logits * scale2 - wide(part(lseb)))
        if masked:
            row = lax.broadcasted_iota(jnp.int32, prob.shape, 0) & (size - 1)
            col = lax.broadcasted_iota(jnp.int32, prob.shape, 1)
            prob = jnp.where(col <= row, prob, 0.0)
        d_prob = dot(part(do), vv, NT)
        score = (prob * (d_prob - wide(part(delb)))).astype(jnp.bfloat16)
        prob = prob.astype(jnp.bfloat16)
        acc[slot, h, 1] += dot(part_t(dot_t), prob, NN)
        acc[slot, h, 0] += dot(part_t(qt), score, NN)
        dq[b, :, first:first + size, :] += dot(score, kk, NN).reshape(heads, size, dim)

    prep(core)
    tile(core, 0, own_slot + core, 0, True)
    tile(core, 1, own_slot + core, 0, False)

    theirs = [
        remote(kv.at[own_slot + other, 0], kv.at[own_slot + other, 0], pair_send.at[0], pair_recv.at[0], {'cp': partner}),
        remote(kv.at[own_slot + other, 1], kv.at[own_slot + other, 1], pair_send.at[1], pair_recv.at[1], {'cp': partner}),
        remote(q.at[other], q.at[other], pair_send.at[2], pair_recv.at[2], {'cp': partner}),
        remote(do.at[other], do.at[other], pair_send.at[3], pair_recv.at[3], {'cp': partner}),
        remote(ld.at[other], ld.at[other], pair_send.at[4], pair_recv.at[4], {'cp': partner}),
    ]
    for copy in theirs:
        copy.wait_recv()

    @pl.when(late_wrap)
    def _():
        kv_send_own(1, last)

    prep(other)
    tile(other, 1, own_slot + other, 1, True)
    tile(1, None, own_slot, core, False)

    swap = remote(acc.at[own_slot + other, 1], rhalf, d_send.at[0], d_recv.at[0], {'cp': partner})
    swap.start()

    def g_copy(slot, h, buf, to_chip):
        return remote(acc.at[slot, h], rbuf.at[buf, h], g_send.at[slot, h], g_recv.at[buf, h], at(to_chip))

    def g_wait(buf, h):
        g_copy(0, h, buf, chip).wait_recv()

    def add_relayed(slot, h):
        g_wait(R, h)
        acc[slot, h] += rbuf[R, h]

    def send_partial(slot, h):
        @pl.when(jnp.logical_and(chip == 1, core == 1))
        def _():
            g_copy(slot, h, A, 0).start()

        @pl.when(chip == 2)
        def _():
            @pl.when(jnp.logical_and(slot == 1, core == 1))
            def _():
                g_copy(slot, h, A, 1).start()

            @pl.when(jnp.logical_and(slot == 0, core == 0))
            def _():
                g_copy(slot, h, R, 1).start()

            @pl.when(jnp.logical_and(slot == 0, core == 1))
            def _():
                g_copy(slot, h, R, 3).start()

        @pl.when(chip == 3)
        def _():
            @pl.when(jnp.logical_and(slot == 0, core == 0))
            def _():
                g_copy(slot, h, B, 0).start()

            @pl.when(jnp.logical_and(slot == 0, core == 1))
            def _():
                add_relayed(slot, h)
                g_copy(slot, h, B, 0).start()

            @pl.when(jnp.logical_and(slot == 1, core == 0))
            def _():
                g_copy(slot, h, R, 2).start()

            @pl.when(jnp.logical_and(slot == 1, core == 1))
            def _():
                g_copy(slot, h, R, 0).start()

            @pl.when(slot == 2)
            def _():
                g_copy(slot, h, A, 2).start()

    @pl.loop(0, chip)
    def _(t):
        slot = jnp.where(jnp.logical_and(chip == last, core == 0), t, chip - 1 - t)
        for copy in kv_copies(slot, own_slot + core, 0, at(chip)):
            copy.wait_recv()

        @pl.when(jnp.logical_and(chip < last, slot == chip - 1))
        def _():
            for copy in kv_copies(slot, slot, 2, at(chip + 1)):
                copy.start()

            @pl.when(late_next)
            def _():
                kv_send_own(0, chip + 1)

        @pl.loop(0, 2)
        def _(h):
            @pl.loop(0, 2)
            def _(b):
                tile(b, None, slot, h, False)

            send_partial(slot, h)

    give_dq = remote(dq.at[other], rdq, d_send.at[1], d_recv.at[1], {'cp': partner})
    give_dq.start()

    relay_add = jnp.logical_and(jnp.logical_or(chip == 1, chip == 2), core == 0)
    relay_pass = jnp.logical_and(chip == 0, core == 1)

    def pass_copy(h):
        return remote(rbuf.at[R, h], rbuf.at[B, h], f_send.at[h], g_recv.at[B, h], at(1))

    for h in range(2):
        @pl.when(relay_add)
        def _():
            add_relayed(chip - 1, h)
            g_copy(chip - 1, h, A, chip - 1).start()

        @pl.when(relay_pass)
        def _():
            g_wait(R, h)
            pass_copy(h).start()

    give_dq.wait_recv()
    for g in range(heads):
        gq[g] = ((dq[core, g] + rdq[g]) * scale).astype(gq.dtype)

    swap.wait_recv()
    from_b = jnp.logical_or(chip == 0, jnp.logical_and(chip == 1, core == 1))
    for h in range(2):
        if h == 1:
            swap_in = rhalf[...]
            swap.wait_send()
            acc[own_slot + core, 1] = swap_in

        @pl.when(chip < last)
        def _():
            g_wait(A, h)
            acc[own_slot + core, h] += rbuf[A, h]

        @pl.when(from_b)
        def _():
            g_wait(B, h)
            acc[own_slot + core, h] += rbuf[B, h]

        gk[h * half:(h + 1) * half, :] = (acc[own_slot + core, h, 0].T * scale).astype(gk.dtype)
        gv[h * half:(h + 1) * half, :] = acc[own_slot + core, h, 1].T.astype(gv.dtype)

    for copy in pair:
        copy.wait_send()
    give_dq.wait_send()

    @pl.when(chip < last)
    def _():
        kv_wait_sent(0)

    @pl.when(chip == 0)
    def _():
        kv_wait_sent(1)

    @pl.when(jnp.logical_and(chip >= 1, chip < last))
    def _():
        kv_wait_sent(2)

    @pl.loop(0, chip)
    def _(slot):
        for h in range(2):
            g_copy(slot, h, A, chip).wait_send()

    @pl.when(relay_pass)
    def _():
        for h in range(2):
            pass_copy(h).wait_send()


def solution(mesh):
    n_dev = mesh.shape['cp']
    row_spec = P(('dp', 'cp'))

    def local_fn(q_tok, k_tok, v_tok, fwd_out, d_out, lse_row):
        rows, heads, dim = q_tok.shape
        half = rows // 2
        row_delta = jnp.einsum('rgd,rgd->rg', d_out, fwd_out, preferred_element_type=jnp.float32)
        row_data = jnp.concatenate(
            [lse_row * LOG2E, row_delta, jnp.zeros((rows, dim - 2 * heads), jnp.float32)], axis=1)
        n_slot = n_dev // 2 + 2
        bf16, f32 = jnp.bfloat16, jnp.float32
        any_spec = pl.BlockSpec(memory_space=pl.ANY)
        vmem_spec = pl.BlockSpec(memory_space=pltpu.VMEM)
        dma = pltpu.SemaphoreType.DMA
        gq, gk, gv = pl.pallas_call(
            functools.partial(kernel, n_dev),
            out_shape=[
                jax.ShapeDtypeStruct((heads, rows, dim), bf16),
                jax.ShapeDtypeStruct((rows, dim), bf16),
                jax.ShapeDtypeStruct((rows, dim), bf16),
            ],
            in_specs=[any_spec] * 5,
            out_specs=[vmem_spec] * 3,
            scratch_shapes=[
                pltpu.VMEM((2, heads, rows, dim), bf16),
                pltpu.VMEM((2, heads, rows, dim), bf16),
                pltpu.VMEM((2, dim, heads * rows), bf16),
                pltpu.VMEM((2, dim, heads * rows), bf16),
                pltpu.VMEM((2, rows, dim), f32),
                pltpu.VMEM((2, heads, rows, dim), f32),
                pltpu.VMEM((2, heads, rows, dim), f32),
                pltpu.VMEM((n_slot, 2, rows, dim), bf16),
                pltpu.VMEM((n_slot, 2, 2, dim, half), f32),
                pltpu.VMEM((2, heads, rows, dim), f32),
                pltpu.VMEM((3, 2, 2, dim, half), f32),
                pltpu.VMEM((2, dim, half), f32),
                pltpu.VMEM((heads, rows, dim), f32),
                dma((5,)), dma((5,)), dma((5,)),
                dma((3, 2)), dma((n_slot, 2)),
                dma((n_slot, 2)), dma((3, 2)), dma((2,)), dma((2,)), dma((2,)),
            ],
            compiler_params=pltpu.CompilerParams(
                collective_id=0, has_side_effects=True, vmem_limit_bytes=62 * 2 ** 20),
            name='attn_bwd',
        )(q_tok.transpose(1, 0, 2), d_out.transpose(1, 0, 2), row_data, k_tok, v_tok)
        return gq.transpose(1, 0, 2), gk, gv

    return jax.shard_map(local_fn, mesh=mesh, in_specs=(row_spec,) * 6, out_specs=(row_spec,) * 3, check_vma=False)
```

time: 288 us -> 74.9 us (0.26)
  the two profiles are of different devices: /device:TPU:112 before, /device:TPU:113 now
where the time goes in v1:
time: 74.9 us; the launch traced here: 74.8 us
  Pallas kernels  67.2 us (90%)
  local copies, waits for them, and re-layouts  4.06 us (5%)
  other arithmetic  2.88 us (4%)
    pallas_call x1, Pallas kernels, local_fn(): pl.pallas_call(functools.partial(kernel, n_dev), out_shape=[jax.ShapeDtyp...  67.2 us
    unnamed x9, local copies, waits for them, and re-layouts  3.54 us
    unnamed x1, other arithmetic  1.87 us

profile of v1, /device:TPU:113, one launch (start us, length us, event | category | flops | bytes accessed | tf_op | source)
XLA Modules:
  0.0 74.8 jit_solution(6039783181365008589)
XLA Ops:
  0.6 0.1 pad.2.clone
  0.7 0.0 copy-start.2
  0.7 1.9 %fusion = f32[1024,3]{0,1:T(4,128)S(1)} fusion(bf16[1024,3,128]{2,0,1:T(8,128)(2,1)} %param.10, bf16[1024,3,128]{2,0,1:T(8,128)(2,1)} %param.9), kind=kLoop, calls=%fused_computation.1 | loop fusion | flops 1569792 | bytes 1585152
  2.6 0.0 copy-done.2
  2.6 0.2 copy.11
  2.8 0.2 copy.16
  3.1 1.0 %maximum_maximum_fusion.ld_hbm = f32[1024,128]{1,0:T(8,128)} fusion(f32[1024,3]{1,0:T(8,128)S(1)} %copy.16, f32[1024,3]{1,0:T(8,128)S(1)} %copy.11, f32[128]{0:T(128)S(1)} %pad.2.clone), kind=kLoop, calls=%fused_computation.2 | loop fusion | flops 262144 | bytes 549376 | tf_op jit(solution)/shard_map/concatenate | solution.py:309
  4.1 67.2 %attn_bwd.1 = (bf16[3,1024,128]{2,1,0:T(8,128)(2,1)}, bf16[1024,128]{1,0:T(8,128)(2,1)}, bf16[1024,128]{1,0:T(8,128)(2,1)}) custom-call(bf16[3,1024,128]{2,1,0:T(8,128)(2,1)} %bitcast.5, bf16[3,1024,128]{2,1,0:T(8,128)(2,1)} %bitcast.3, f32[1024,128]{1,0:T(8,128)} %maximum_maximum_fusion.ld_hbm, bf16[1024,128]{1,0:T(8,128)(2,1)} %k_hbm.1, ...), custom_call_target="tpu_custom_call" | custom-call | tf_op jit(solution)/shard_map/attn_bwd/pallas_call | solution.py:316
  71.2 0.0 copy-start.1
  71.3 0.0 copy-start
  71.3 2.1 %copy.21 = bf16[1024,3,128]{2,0,1:T(8,128)(2,1)} copy(bf16[1024,3,128]{2,0,1:T(8,128)(2,1)} %bitcast.4) | data formatting | bytes 1572864
  73.4 0.0 copy-done.1
  73.4 0.7 copy.22
  74.1 0.0 copy-done
  74.1 0.7 copy.23
  (2 shorter events, 0.0 us)
Async XLA Ops:
  0.7 1.9 %copy-start.2 = (f32[1024,3]{0,1:T(4,128)S(1)}, f32[1024,3]{0,1:T(4,128)}, u32[]{:S(2)}) copy-start(f32[1024,3]{0,1:T(4,128)} %param.11) | copy-start | bytes 36868
  71.2 2.1 %copy-start.1 = (bf16[1024,128]{1,0:T(8,128)(2,1)S(1)}, bf16[1024,128]{1,0:T(8,128)(2,1)}, u32[]{:S(2)}) copy-start(bf16[1024,128]{1,0:T(8,128)(2,1)} %get-tuple-element.13) | copy-start | bytes 786436
  71.3 2.8 %copy-start = (bf16[1024,128]{1,0:T(8,128)(2,1)S(1)}, bf16[1024,128]{1,0:T(8,128)(2,1)}, u32[]{:S(2)}) copy-start(bf16[1024,128]{1,0:T(8,128)(2,1)} %get-tuple-element.14) | copy-start | bytes 786436

commit v2 on v1

--- a/solution.py
+++ b/solution.py
@@ -18,9 +18,9 @@
     return lax.dot_general(a, b, dims, preferred_element_type=jnp.float32)
 
 
-def kernel(n_dev, q_hbm, do_hbm, ld_hbm, k_hbm, v_hbm, gq, gk, gv,
-           q, do, qt, dot_t, ld, lseb, delb, kv, acc, dq, rbuf, rhalf, rdq,
-           in_sem, pair_send, pair_recv, kv_send, kv_recv, g_send, g_recv, f_send, d_send, d_recv):
+def kernel(n_dev, q_hbm, do_hbm, fo_hbm, lse_hbm, k_hbm, v_hbm, out_hbm,
+           q, do, fo, lse, qt, dot_t, lseb, delb, kv, acc, dq, rbuf, rhalf, rdq, out,
+           in_sem, pair_send, pair_recv, kv_send, kv_recv, g_send, g_recv, f_send, d_send, d_recv, out_sem):
     heads, rows, dim = q.shape[1:]
     half = rows // 2
     scale = dim ** -0.5
@@ -41,7 +41,8 @@
         pltpu.make_async_copy(v_hbm, kv.at[own_slot + core, 1], in_sem.at[1]),
         pltpu.make_async_copy(q_hbm, q.at[core], in_sem.at[2]),
         pltpu.make_async_copy(do_hbm, do.at[core], in_sem.at[3]),
-        pltpu.make_async_copy(ld_hbm, ld.at[core], in_sem.at[4]),
+        pltpu.make_async_copy(fo_hbm, fo.at[core], in_sem.at[4]),
+        pltpu.make_async_copy(lse_hbm, lse.at[core], in_sem.at[5]),
     ]
     for copy in loads:
         copy.start()
@@ -83,14 +84,12 @@
     def _():
         kv_send_own(1, last)
 
-    pair = [
-        remote(kv.at[own_slot + core, 0], kv.at[own_slot + core, 0], pair_send.at[0], pair_recv.at[0], {'cp': partner}),
-        remote(kv.at[own_slot + core, 1], kv.at[own_slot + core, 1], pair_send.at[1], pair_recv.at[1], {'cp': partner}),
-        remote(q.at[core], q.at[core], pair_send.at[2], pair_recv.at[2], {'cp': partner}),
-        remote(do.at[core], do.at[core], pair_send.at[3], pair_recv.at[3], {'cp': partner}),
-        remote(ld.at[core], ld.at[core], pair_send.at[4], pair_recv.at[4], {'cp': partner}),
-    ]
-    for i in (2, 3, 4):
+    def pair_copies(c):
+        refs = (kv.at[own_slot + c, 0], kv.at[own_slot + c, 1], q.at[c], do.at[c], fo.at[c], lse.at[c])
+        return [remote(ref, ref, pair_send.at[i], pair_recv.at[i], {'cp': partner}) for i, ref in enumerate(refs)]
+
+    pair = pair_copies(core)
+    for i in (2, 3, 4, 5):
         loads[i].wait()
         pair[i].start()
     pair[0].start()
@@ -100,8 +99,9 @@
         qt[b] = q[b].reshape(heads * rows, dim).T
         dot_t[b] = do[b].reshape(heads * rows, dim).T
         for g in range(heads):
-            lseb[b, g] = jnp.broadcast_to(ld[b, :, g:g + 1], (rows, dim))
-            delb[b, g] = jnp.broadcast_to(ld[b, :, heads + g:heads + g + 1], (rows, dim))
+            lseb[b, g] = jnp.broadcast_to(lse[b, g:g + 1, :] * LOG2E, (dim, rows)).T
+            delta = jnp.sum(do[b, g].astype(jnp.float32) * fo[b, g].astype(jnp.float32), axis=1, keepdims=True)
+            delb[b, g] = jnp.broadcast_to(delta, (rows, dim))
 
     def tile(b, row_half, slot, h, masked):
         size = rows if row_half is None else half
@@ -130,14 +130,7 @@
     tile(core, 0, own_slot + core, 0, True)
     tile(core, 1, own_slot + core, 0, False)
 
-    theirs = [
-        remote(kv.at[own_slot + other, 0], kv.at[own_slot + other, 0], pair_send.at[0], pair_recv.at[0], {'cp': partner}),
-        remote(kv.at[own_slot + other, 1], kv.at[own_slot + other, 1], pair_send.at[1], pair_recv.at[1], {'cp': partner}),
-        remote(q.at[other], q.at[other], pair_send.at[2], pair_recv.at[2], {'cp': partner}),
-        remote(do.at[other], do.at[other], pair_send.at[3], pair_recv.at[3], {'cp': partner}),
-        remote(ld.at[other], ld.at[other], pair_send.at[4], pair_recv.at[4], {'cp': partner}),
-    ]
-    for copy in theirs:
+    for copy in pair_copies(other):
         copy.wait_recv()
 
     @pl.when(late_wrap)
@@ -145,11 +138,6 @@
         kv_send_own(1, last)
 
     prep(other)
-    tile(other, 1, own_slot + other, 1, True)
-    tile(1, None, own_slot, core, False)
-
-    swap = remote(acc.at[own_slot + other, 1], rhalf, d_send.at[0], d_recv.at[0], {'cp': partner})
-    swap.start()
 
     def g_copy(slot, h, buf, to_chip):
         return remote(acc.at[slot, h], rbuf.at[buf, h], g_send.at[slot, h], g_recv.at[buf, h], at(to_chip))
@@ -226,8 +214,27 @@
 
             send_partial(slot, h)
 
+    swap = remote(acc.at[own_slot + other, 1], rhalf, d_send.at[0], d_recv.at[0], {'cp': partner})
     give_dq = remote(dq.at[other], rdq, d_send.at[1], d_recv.at[1], {'cp': partner})
-    give_dq.start()
+    tile(other, 1, own_slot + other, 1, True)
+
+    @pl.when(core == 0)
+    def _():
+        swap.start()
+
+    @pl.when(core == 1)
+    def _():
+        give_dq.start()
+
+    tile(1, None, own_slot, core, False)
+
+    @pl.when(core == 1)
+    def _():
+        swap.start()
+
+    @pl.when(core == 0)
+    def _():
+        give_dq.start()
 
     relay_add = jnp.logical_and(jnp.logical_or(chip == 1, chip == 2), core == 0)
     relay_pass = jnp.logical_and(chip == 0, core == 1)
@@ -248,7 +255,14 @@
 
     give_dq.wait_recv()
     for g in range(heads):
-        gq[g] = ((dq[core, g] + rdq[g]) * scale).astype(gq.dtype)
+        out[g] = ((dq[core, g] + rdq[g]) * scale).astype(out.dtype)
+    stores = [pltpu.make_async_copy(out.at[0:heads], out_hbm.at[0:heads], out_sem.at[0])]
+    for h in range(2):
+        span = pl.ds(h * half, half)
+        for i in range(2):
+            stores.append(pltpu.make_async_copy(
+                out.at[heads + i, span], out_hbm.at[heads + i, span], out_sem.at[1 + 2 * h + i]))
+    stores[0].start()
 
     swap.wait_recv()
     from_b = jnp.logical_or(chip == 0, jnp.logical_and(chip == 1, core == 1))
@@ -268,8 +282,10 @@
             g_wait(B, h)
             acc[own_slot + core, h] += rbuf[B, h]
 
-        gk[h * half:(h + 1) * half, :] = (acc[own_slot + core, h, 0].T * scale).astype(gk.dtype)
-        gv[h * half:(h + 1) * half, :] = acc[own_slot + core, h, 1].T.astype(gv.dtype)
+        out[heads, h * half:(h + 1) * half, :] = (acc[own_slot + core, h, 0].T * scale).astype(out.dtype)
+        out[heads + 1, h * half:(h + 1) * half, :] = acc[own_slot + core, h, 1].T.astype(out.dtype)
+        stores[1 + 2 * h].start()
+        stores[2 + 2 * h].start()
 
     for copy in pair:
         copy.wait_send()
@@ -297,6 +313,24 @@
         for h in range(2):
             pass_copy(h).wait_send()
 
+    for copy in stores:
+        copy.wait()
+
+
+def unpack_kernel(packed, gq, gk, gv, held, in_sem, out_sem):
+    heads = gq.shape[0]
+    n = packed.shape[0]
+    reads = [pltpu.make_async_copy(packed.at[i], held.at[i], in_sem.at[i]) for i in range(n)]
+    outs = [gq.at[i] for i in range(heads)] + [gk, gv]
+    writes = [pltpu.make_async_copy(held.at[i], outs[i], out_sem.at[i]) for i in range(n)]
+    for copy in reads:
+        copy.start()
+    for read, write in zip(reads, writes):
+        read.wait()
+        write.start()
+    for copy in writes:
+        copy.wait()
+
 
 def solution(mesh):
     n_dev = mesh.shape['cp']
@@ -305,29 +339,22 @@
     def local_fn(q_tok, k_tok, v_tok, fwd_out, d_out, lse_row):
         rows, heads, dim = q_tok.shape
         half = rows // 2
-        row_delta = jnp.einsum('rgd,rgd->rg', d_out, fwd_out, preferred_element_type=jnp.float32)
-        row_data = jnp.concatenate(
-            [lse_row * LOG2E, row_delta, jnp.zeros((rows, dim - 2 * heads), jnp.float32)], axis=1)
         n_slot = n_dev // 2 + 2
         bf16, f32 = jnp.bfloat16, jnp.float32
         any_spec = pl.BlockSpec(memory_space=pl.ANY)
-        vmem_spec = pl.BlockSpec(memory_space=pltpu.VMEM)
         dma = pltpu.SemaphoreType.DMA
-        gq, gk, gv = pl.pallas_call(
+        packed = pl.pallas_call(
             functools.partial(kernel, n_dev),
-            out_shape=[
-                jax.ShapeDtypeStruct((heads, rows, dim), bf16),
-                jax.ShapeDtypeStruct((rows, dim), bf16),
-                jax.ShapeDtypeStruct((rows, dim), bf16),
-            ],
-            in_specs=[any_spec] * 5,
-            out_specs=[vmem_spec] * 3,
+            out_shape=jax.ShapeDtypeStruct((heads + 2, rows, dim), bf16),
+            in_specs=[any_spec] * 6,
+            out_specs=any_spec,
             scratch_shapes=[
                 pltpu.VMEM((2, heads, rows, dim), bf16),
                 pltpu.VMEM((2, heads, rows, dim), bf16),
+                pltpu.VMEM((2, heads, rows, dim), bf16),
+                pltpu.VMEM((2, heads, rows), f32),
                 pltpu.VMEM((2, dim, heads * rows), bf16),
                 pltpu.VMEM((2, dim, heads * rows), bf16),
-                pltpu.VMEM((2, rows, dim), f32),
                 pltpu.VMEM((2, heads, rows, dim), f32),
                 pltpu.VMEM((2, heads, rows, dim), f32),
                 pltpu.VMEM((n_slot, 2, rows, dim), bf16),
@@ -336,14 +363,27 @@
                 pltpu.VMEM((3, 2, 2, dim, half), f32),
                 pltpu.VMEM((2, dim, half), f32),
                 pltpu.VMEM((heads, rows, dim), f32),
-                dma((5,)), dma((5,)), dma((5,)),
+                pltpu.VMEM((heads + 2, rows, dim), bf16),
+                dma((6,)), dma((6,)), dma((6,)),
                 dma((3, 2)), dma((n_slot, 2)),
-                dma((n_slot, 2)), dma((3, 2)), dma((2,)), dma((2,)), dma((2,)),
+                dma((n_slot, 2)), dma((3, 2)), dma((2,)), dma((2,)), dma((2,)), dma((5,)),
             ],
             compiler_params=pltpu.CompilerParams(
                 collective_id=0, has_side_effects=True, vmem_limit_bytes=62 * 2 ** 20),
             name='attn_bwd',
-        )(q_tok.transpose(1, 0, 2), d_out.transpose(1, 0, 2), row_data, k_tok, v_tok)
+        )(q_tok.transpose(1, 0, 2), d_out.transpose(1, 0, 2), fwd_out.transpose(1, 0, 2), lse_row.T, k_tok, v_tok)
+        gq, gk, gv = pl.pallas_call(
+            unpack_kernel,
+            out_shape=[
+                jax.ShapeDtypeStruct((heads, rows, dim), bf16),
+                jax.ShapeDtypeStruct((rows, dim), bf16),
+                jax.ShapeDtypeStruct((rows, dim), bf16),
+            ],
+            in_specs=[any_spec],
+            out_specs=[any_spec] * 3,
+            scratch_shapes=[pltpu.VMEM((heads + 2, rows, dim), bf16), dma((heads + 2,)), dma((heads + 2,))],
+            name='unpack',
+        )(packed)
         return gq.transpose(1, 0, 2), gk, gv
 
     return jax.shard_map(local_fn, mesh=mesh, in_specs=(row_spec,) * 6, out_specs=(row_spec,) * 3, check_vma=False)

time: 74.9 us -> 69.9 us (0.933)
  local copies, waits for them, and re-layouts: 4.06 us -> 0 us
  other arithmetic: 2.88 us -> 0 us
  Pallas kernels: 67.2 us -> 68.9 us
    unnamed x9 -> x0, local copies, waits for them, and re-layouts: 3.54 us -> none
    unnamed x1 -> x0, other arithmetic: 1.87 us -> none
    pallas_call x1 -> x2, Pallas kernels: 67.2 us -> 68.9 us  [the longest x1 66.9 us: local_fn(): pl.pallas_call(functools.partial(kernel, n_dev), out_shape=jax.ShapeDtype...]
    concatenate x1 -> x0, other arithmetic: 1.01 us -> none  [local_fn(): jnp.concatenate([lse_row * LOG2E, row_delta, jnp.zeros((rows, dim - 2 * h...]
where the time goes in v2:
time: 69.9 us; the launch traced here: 69.8 us
  Pallas kernels  68.9 us (99%)
  between operations  0.8 us (1%)
    pallas_call x1, Pallas kernels, local_fn(): pl.pallas_call(functools.partial(kernel, n_dev), out_shape=jax.ShapeDtype...  66.9 us
    pallas_call x1, Pallas kernels, local_fn(): pl.pallas_call(unpack_kernel, out_shape=[jax.ShapeDtypeStruct((heads, row...  2.08 us

profile of v2, /device:TPU:113, one launch (start us, length us, event | category | flops | bytes accessed | tf_op | source)
XLA Modules:
  0.0 69.8 jit_solution(11811928247332996040)
XLA Ops:
  0.6 66.9 %attn_bwd.1.packed = bf16[5,1024,128]{2,1,0:T(8,128)(2,1)} custom-call(bf16[3,1024,128]{2,1,0:T(8,128)(2,1)} %bitcast.5, bf16[3,1024,128]{2,1,0:T(8,128)(2,1)} %bitcast.6, bf16[3,1024,128]{2,1,0:T(8,128)(2,1)} %bitcast.7, f32[3,1024]{1,0:T(4,128)} %bitcast.8, bf16[1024,128]{1,0:T(8,128)(2,1)} %k_hbm.1, bf16[1024,128]{1,0:T(8,128)(2,1)} %v_hbm.1), custom_call_target="tpu_custom_call" | custom-call | tf_op jit(solution)/shard_map/attn_bwd/pallas_call | solution.py:346
  67.5 2.1 %unpack.1 = (bf16[3,1024,128]{2,1,0:T(8,128)(2,1)}, bf16[1024,128]{1,0:T(8,128)(2,1)}, bf16[1024,128]{1,0:T(8,128)(2,1)}) custom-call(bf16[5,1024,128]{2,1,0:T(8,128)(2,1)} %attn_bwd.1.packed), custom_call_target="tpu_custom_call" | custom-call | tf_op jit(solution)/shard_map/unpack/pallas_call | solution.py:375

commit v3 on v2

v3 whole, which is shorter than its diff:
```python
import functools
import math

import jax
import jax.numpy as jnp
from jax import lax
from jax.experimental import pallas as pl
from jax.experimental.pallas import tpu as pltpu
from jax.sharding import PartitionSpec as P

NT = (((1,), (1,)), ((), ()))
NN = (((1,), (0,)), ((), ()))
LOG2E = math.log2(math.e)
A, B, R = 0, 1, 2


def dot(a, b, dims):
    return lax.dot_general(a, b, dims, preferred_element_type=jnp.float32)


def kernel(n_dev, q_hbm, do_hbm, fo_hbm, lse_hbm, k_hbm, v_hbm, out_hbm,
           q, do, fo, lse, stats, qt, dot_t, lseb, delb, kv, acc, dq, rbuf, rhalf, rdq, out,
           guest_q, guest_do, guest_stats, guest_qt, guest_dot, guest_lse, guest_del, guest_dq, back_dq,
           in_sem, pair_send, pair_recv, kv_send, kv_recv, g_send, g_recv, f_send, d_send, d_recv,
           guest_send, guest_recv, out_sem):
    heads, rows, dim = q.shape[1:]
    half = rows // 2
    scale = dim ** -0.5
    scale2 = scale * LOG2E
    own_slot = n_dev // 2
    n_chip = n_dev // 2
    last = n_chip - 1

    me = lax.axis_index('cp')
    chip, core = me // 2, me % 2
    other = 1 - core
    partner = {'cp': chip * 2 + other}

    def at(chip_id):
        return {'cp': chip_id * 2 + core}

    loads = [
        pltpu.make_async_copy(k_hbm, kv.at[own_slot + core, 0], in_sem.at[0]),
        pltpu.make_async_copy(v_hbm, kv.at[own_slot + core, 1], in_sem.at[1]),
        pltpu.make_async_copy(q_hbm, q.at[core], in_sem.at[2]),
        pltpu.make_async_copy(do_hbm, do.at[core], in_sem.at[3]),
        pltpu.make_async_copy(fo_hbm, fo, in_sem.at[4]),
        pltpu.make_async_copy(lse_hbm, lse, in_sem.at[5]),
    ]
    for copy in loads:
        copy.start()

    barrier = pltpu.get_barrier_semaphore()
    for d in range(1, n_dev):
        pl.semaphore_signal(barrier, inc=1, device_id={'cp': lax.rem(me + d, n_dev)}, device_id_type=pl.DeviceIdType.MESH)
    acc[...] = jnp.zeros_like(acc)
    dq[...] = jnp.zeros_like(dq)
    pl.semaphore_wait(barrier, n_dev - 1)

    def remote(src, dst, send, recv, device):
        return pltpu.make_async_remote_copy(src_ref=src, dst_ref=dst, send_sem=send, recv_sem=recv,
                                            device_id=device, device_id_type=pl.DeviceIdType.MESH)

    def kv_copies(slot, src_slot, h, sem_row, device):
        span = pl.ds(h * half, half)
        return [remote(kv.at[src_slot, i, span], kv.at[slot, i, span],
                       kv_send.at[sem_row, h, i], kv_recv.at[slot, h, i], device) for i in range(2)]

    def kv_send_own(sem_row, to_chip):
        for h in range(2):
            for copy in kv_copies(chip, own_slot + core, h, sem_row, at(to_chip)):
                copy.start()

    def kv_wait_sent(sem_row):
        for h in range(2):
            for copy in kv_copies(0, 0, h, sem_row, at(chip)):
                copy.wait_send()

    late_next = jnp.logical_and(chip == last - 1, core == 0)
    late_wrap = jnp.logical_and(chip == 0, core == 1)
    loads[0].wait()
    loads[1].wait()

    @pl.when(jnp.logical_and(chip < last, jnp.logical_not(late_next)))
    def _():
        kv_send_own(0, chip + 1)

    @pl.when(jnp.logical_and(chip == 0, core == 0))
    def _():
        kv_send_own(1, last)

    def pair_copies(c):
        refs = (q.at[c], do.at[c], kv.at[own_slot + c, 0], kv.at[own_slot + c, 1], stats.at[c])
        return [remote(ref, ref, pair_send.at[i], pair_recv.at[i], partner) for i, ref in enumerate(refs)]

    guest_rows = pl.ds(half, half)
    guests = [
        remote(q.at[core, :, guest_rows], guest_q, guest_send.at[0], guest_recv.at[0], at(0)),
        remote(do.at[core, :, guest_rows], guest_do, guest_send.at[1], guest_recv.at[1], at(0)),
        remote(stats.at[core, :, guest_rows], guest_stats, guest_send.at[2], guest_recv.at[2], at(0)),
    ]
    guests_back = remote(guest_dq, back_dq, d_send.at[2], d_recv.at[2], at(last))

    pair = pair_copies(core)
    for i in (2, 3):
        loads[i].wait()

        @pl.when(chip == last)
        def _():
            guests[i - 2].start()

        pair[i - 2].start()
    pair[2].start()
    pair[3].start()
    loads[4].wait()
    loads[5].wait()
    for g in range(heads):
        stats[core, g:g + 1, :] = lse[g:g + 1, :] * LOG2E
        product = do[core, g].astype(jnp.float32) * fo[g].astype(jnp.float32)
        stats[core, heads + g:heads + g + 1, :] = jnp.sum(product.T, axis=0, keepdims=True)
    pair[4].start()

    @pl.when(chip == last)
    def _():
        guests[2].start()

    def spread(row):
        return jnp.broadcast_to(row, (dim, row.shape[1])).T

    def prep(b):
        qt[b] = q[b].reshape(heads * rows, dim).T
        dot_t[b] = do[b].reshape(heads * rows, dim).T
        for g in range(heads):
            lseb[b, g] = spread(stats[b, g:g + 1, :])
            delb[b, g] = spread(stats[b, heads + g:heads + g + 1, :])

    def pair_grads(q_rows, do_rows, q_cols, do_cols, lse_rows, del_rows, kk, vv, size, masked):
        wide = lambda x: jnp.concatenate([x] * (kk.shape[0] // dim), axis=1)
        logits = dot(q_rows, kk, NT)
        prob = jnp.exp2(logits * scale2 - wide(lse_rows))
        if masked:
            row = lax.broadcasted_iota(jnp.int32, prob.shape, 0) & (size - 1)
            col = lax.broadcasted_iota(jnp.int32, prob.shape, 1)
            prob = jnp.where(col <= row, prob, 0.0)
        d_prob = dot(do_rows, vv, NT)
        score = (prob * (d_prob - wide(del_rows))).astype(jnp.bfloat16)
        prob = prob.astype(jnp.bfloat16)
        return dot(q_cols, score, NN), dot(do_cols, prob, NN), dot(score, kk, NN)

    def tile(blocks, first, size, slot, h, masked=False):
        start = pl.multiple_of(h * half, half)
        kk = kv[slot, 0, pl.ds(start, half), :]
        vv = kv[slot, 1, pl.ds(start, half), :]
        part = lambda ref: jnp.concatenate(
            [ref[b, :, first:first + size, :].reshape(heads * size, dim) for b in blocks], axis=0)
        part_t = lambda ref: jnp.concatenate(
            [ref[b, :, g * rows + first:g * rows + first + size] for b in blocks for g in range(heads)], axis=1)
        d_key, d_value, d_query = pair_grads(
            part(q), part(do), part_t(qt), part_t(dot_t), part(lseb), part(delb), kk, vv, size, masked)
        acc[slot, h, 0] += d_key
        acc[slot, h, 1] += d_value
        for i, b in enumerate(blocks):
            n = heads * size
            dq[b, :, first:first + size, :] += d_query[i * n:(i + 1) * n].reshape(heads, size, dim)

    prep(core)
    tile((core,), 0, half, own_slot + core, 0, masked=True)
    tile((core,), half, half, own_slot + core, 0)

    for copy in pair_copies(other):
        copy.wait_recv()

    @pl.when(late_wrap)
    def _():
        kv_send_own(1, last)

    prep(other)

    @pl.when(chip == 0)
    def _():
        for copy in guests:
            copy.wait_recv()
        n = heads * half
        guest_qt[...] = guest_q[...].reshape(n, dim).T
        guest_dot[...] = guest_do[...].reshape(n, dim).T
        for g in range(heads):
            guest_lse[g] = spread(guest_stats[g:g + 1, :])
            guest_del[g] = spread(guest_stats[heads + g:heads + g + 1, :])
        guest_dq[...] = jnp.zeros_like(guest_dq)

        @pl.loop(0, 2)
        def _(b):
            flat = lambda ref: ref[...].reshape(n, dim)
            d_key, d_value, d_query = pair_grads(
                flat(guest_q), flat(guest_do), guest_qt[...], guest_dot[...], flat(guest_lse), flat(guest_del),
                kv[own_slot + b, 0], kv[own_slot + b, 1], half, False)
            for h in range(2):
                acc[own_slot + b, h, 0] += d_key[:, h * half:(h + 1) * half]
                acc[own_slot + b, h, 1] += d_value[:, h * half:(h + 1) * half]
            guest_dq[...] += d_query.reshape(heads, half, dim)

        guests_back.start()

    def g_copy(slot, h, buf, to_chip):
        return remote(acc.at[slot, h], rbuf.at[buf, h], g_send.at[slot, h], g_recv.at[buf, h], at(to_chip))

    def g_wait(buf, h):
        g_copy(0, h, buf, chip).wait_recv()

    def add_relayed(slot, h):
        g_wait(R, h)
        acc[slot, h] += rbuf[R, h]

    def send_partial(slot, h):
        @pl.when(jnp.logical_and(chip == 1, core == 1))
        def _():
            g_copy(slot, h, A, 0).start()

        @pl.when(chip == 2)
        def _():
            @pl.when(jnp.logical_and(slot == 1, core == 1))
            def _():
                g_copy(slot, h, A, 1).start()

            @pl.when(jnp.logical_and(slot == 0, core == 0))
            def _():
                g_copy(slot, h, R, 1).start()

            @pl.when(jnp.logical_and(slot == 0, core == 1))
            def _():
                g_copy(slot, h, R, 3).start()

        @pl.when(chip == 3)
        def _():
            @pl.when(jnp.logical_and(slot == 0, core == 0))
            def _():
                g_copy(slot, h, B, 0).start()

            @pl.when(jnp.logical_and(slot == 0, core == 1))
            def _():
                add_relayed(slot, h)
                g_copy(slot, h, B, 0).start()

            @pl.when(jnp.logical_and(slot == 1, core == 0))
            def _():
                g_copy(slot, h, R, 2).start()

            @pl.when(jnp.logical_and(slot == 1, core == 1))
            def _():
                g_copy(slot, h, R, 0).start()

            @pl.when(slot == 2)
            def _():
                g_copy(slot, h, A, 2).start()

    @pl.loop(0, chip)
    def _(t):
        slot = jnp.where(jnp.logical_and(chip == last, core == 0), t, chip - 1 - t)

        @pl.loop(0, 2)
        def _(h):
            for copy in kv_copies(slot, own_slot + core, h, 0, at(chip)):
                copy.wait_recv()

            @pl.when(jnp.logical_and(chip < last, slot == chip - 1))
            def _():
                for copy in kv_copies(slot, slot, h, 2, at(chip + 1)):
                    copy.start()

                @pl.when(jnp.logical_and(late_next, h == 1))
                def _():
                    kv_send_own(0, chip + 1)

            with_guests = jnp.logical_and(chip == last, slot == 0)

            @pl.when(with_guests)
            def _():
                tile((0, 1), 0, half, slot, h)

            @pl.when(jnp.logical_not(with_guests))
            def _():
                @pl.loop(0, 2)
                def _(b):
                    tile((b,), 0, rows, slot, h)

            send_partial(slot, h)

    relay_add = jnp.logical_and(jnp.logical_or(chip == 1, chip == 2), core == 0)
    relay_pass = jnp.logical_and(chip == 0, core == 1)

    def pass_copy(h):
        return remote(rbuf.at[R, h], rbuf.at[B, h], f_send.at[h], g_recv.at[B, h], at(1))

    def relay(h):
        @pl.when(relay_add)
        def _():
            add_relayed(chip - 1, h)
            g_copy(chip - 1, h, A, chip - 1).start()

    swaps = [remote(acc.at[own_slot + other, h], rhalf.at[h], d_send.at[3 * h], d_recv.at[3 * h], partner)
             for h in range(2)]
    give_dq = remote(dq.at[other], rdq, d_send.at[1], d_recv.at[1], partner)

    relay(0)
    tile((other,), half, half, own_slot + other, 1, masked=True)

    @pl.when(core == 0)
    def _():
        swaps[1].start()

    @pl.when(core == 1)
    def _():
        give_dq.start()

    relay(1)
    tile((1,), 0, rows, own_slot, core)

    @pl.when(core == 1)
    def _():
        swaps[1].start()

    @pl.when(core == 0)
    def _():
        give_dq.start()

    @pl.when(chip == 0)
    def _():
        swaps[0].start()

    give_dq.wait_recv()
    for g in range(heads):
        out[g] = ((dq[core, g] + rdq[g]) * scale).astype(out.dtype)

    @pl.when(chip == last)
    def _():
        guests_back.wait_recv()
        for g in range(heads):
            out[g, half:, :] = ((dq[core, g, half:, :] + rdq[g, half:, :] + back_dq[g]) * scale).astype(out.dtype)

    stores = [pltpu.make_async_copy(out.at[0:heads], out_hbm.at[0:heads], out_sem.at[0])]
    for h in range(2):
        span = pl.ds(h * half, half)
        for i in range(2):
            stores.append(pltpu.make_async_copy(
                out.at[heads + i, span], out_hbm.at[heads + i, span], out_sem.at[1 + 2 * h + i]))
    stores[0].start()

    @pl.when(relay_pass)
    def _():
        for h in range(2):
            g_wait(R, h)
            pass_copy(h).start()

    @pl.when(chip == 0)
    def _():
        swaps[0].wait_recv()
        acc[own_slot + core, 0] += rhalf[0]

    swaps[1].wait_recv()
    acc[own_slot + core, 1] += rhalf[1]
    from_b = jnp.logical_or(chip == 0, jnp.logical_and(chip == 1, core == 1))
    for h in range(2):
        @pl.when(chip < last)
        def _():
            g_wait(A, h)
            acc[own_slot + core, h] += rbuf[A, h]

        @pl.when(from_b)
        def _():
            g_wait(B, h)
            acc[own_slot + core, h] += rbuf[B, h]

        out[heads, h * half:(h + 1) * half, :] = (acc[own_slot + core, h, 0].T * scale).astype(out.dtype)
        out[heads + 1, h * half:(h + 1) * half, :] = acc[own_slot + core, h, 1].T.astype(out.dtype)
        stores[1 + 2 * h].start()
        stores[2 + 2 * h].start()

    for copy in pair:
        copy.wait_send()
    give_dq.wait_send()
    swaps[1].wait_send()

    @pl.when(chip == 0)
    def _():
        swaps[0].wait_send()
        guests_back.wait_send()
        kv_wait_sent(1)

    @pl.when(chip == last)
    def _():
        for copy in guests:
            copy.wait_send()

    @pl.when(chip < last)
    def _():
        kv_wait_sent(0)

    @pl.when(jnp.logical_and(chip >= 1, chip < last))
    def _():
        kv_wait_sent(2)

    @pl.loop(0, chip)
    def _(slot):
        for h in range(2):
            g_copy(slot, h, A, chip).wait_send()

    @pl.when(relay_pass)
    def _():
        for h in range(2):
            pass_copy(h).wait_send()

    for copy in stores:
        copy.wait()


def unpack_kernel(packed, gq, gk, gv, held, in_sem, out_sem):
    heads = gq.shape[0]
    n = packed.shape[0]
    reads = [pltpu.make_async_copy(packed.at[i], held.at[i], in_sem.at[i]) for i in range(n)]
    outs = [gq.at[i] for i in range(heads)] + [gk, gv]
    writes = [pltpu.make_async_copy(held.at[i], outs[i], out_sem.at[i]) for i in range(n)]
    for copy in reads:
        copy.start()
    for read, write in zip(reads, writes):
        read.wait()
        write.start()
    for copy in writes:
        copy.wait()


def solution(mesh):
    n_dev = mesh.shape['cp']
    row_spec = P(('dp', 'cp'))

    def local_fn(q_tok, k_tok, v_tok, fwd_out, d_out, lse_row):
        rows, heads, dim = q_tok.shape
        half = rows // 2
        n_slot = n_dev // 2 + 2
        bf16, f32 = jnp.bfloat16, jnp.float32
        any_spec = pl.BlockSpec(memory_space=pl.ANY)
        dma = pltpu.SemaphoreType.DMA
        vmem = pltpu.VMEM
        packed = pl.pallas_call(
            functools.partial(kernel, n_dev),
            out_shape=jax.ShapeDtypeStruct((heads + 2, rows, dim), bf16),
            in_specs=[any_spec] * 6,
            out_specs=any_spec,
            scratch_shapes=[
                vmem((2, heads, rows, dim), bf16), vmem((2, heads, rows, dim), bf16),
                vmem((heads, rows, dim), bf16), vmem((heads, rows), f32), vmem((2, 8, rows), f32),
                vmem((2, dim, heads * rows), bf16), vmem((2, dim, heads * rows), bf16),
                vmem((2, heads, rows, dim), f32), vmem((2, heads, rows, dim), f32),
                vmem((n_slot, 2, rows, dim), bf16),
                vmem((n_slot, 2, 2, dim, half), f32),
                vmem((2, heads, rows, dim), f32),
                vmem((3, 2, 2, dim, half), f32), vmem((2, 2, dim, half), f32),
                vmem((heads, rows, dim), f32),
                vmem((heads + 2, rows, dim), bf16),
                vmem((heads, half, dim), bf16), vmem((heads, half, dim), bf16), vmem((8, half), f32),
                vmem((dim, heads * half), bf16), vmem((dim, heads * half), bf16),
                vmem((heads, half, dim), f32), vmem((heads, half, dim), f32),
                vmem((heads, half, dim), f32), vmem((heads, half, dim), f32),
                dma((6,)), dma((5,)), dma((5,)),
                dma((3, 2, 2)), dma((n_slot, 2, 2)),
                dma((n_slot, 2)), dma((3, 2)), dma((2,)), dma((4,)), dma((4,)),
                dma((3,)), dma((3,)), dma((5,)),
            ],
            compiler_params=pltpu.CompilerParams(
                collective_id=0, has_side_effects=True, vmem_limit_bytes=62 * 2 ** 20),
            name='attn_bwd',
        )(q_tok.transpose(1, 0, 2), d_out.transpose(1, 0, 2), fwd_out.transpose(1, 0, 2), lse_row.T, k_tok, v_tok)
        gq, gk, gv = pl.pallas_call(
            unpack_kernel,
            out_shape=[
                jax.ShapeDtypeStruct((heads, rows, dim), bf16),
                jax.ShapeDtypeStruct((rows, dim), bf16),
                jax.ShapeDtypeStruct((rows, dim), bf16),
            ],
            in_specs=[any_spec],
            out_specs=[any_spec] * 3,
            scratch_shapes=[pltpu.VMEM((heads + 2, rows, dim), bf16), dma((heads + 2,)), dma((heads + 2,))],
            name='unpack',
        )(packed)
        return gq.transpose(1, 0, 2), gk, gv

    return jax.shard_map(local_fn, mesh=mesh, in_specs=(row_spec,) * 6, out_specs=(row_spec,) * 3, check_vma=False)
```

time: 69.9 us -> 63.1 us (0.903); the launches traced: 69.8 us -> 61.9 us
  Pallas kernels: 68.9 us -> 61.1 us
    pallas_call x1, Pallas kernels: 66.9 us -> 59 us  [local_fn(): pl.pallas_call(functools.partial(kernel, n_dev), out_shape=jax.ShapeDtype...]
where the time goes in v3:
time: 63.1 us; the launch traced here: 61.9 us
  Pallas kernels  61.1 us (97%)
  between operations  0.82 us (1%)
    pallas_call x1, Pallas kernels, local_fn(): pl.pallas_call(functools.partial(kernel, n_dev), out_shape=jax.ShapeDtype...  59 us
    pallas_call x1, Pallas kernels, local_fn(): pl.pallas_call(unpack_kernel, out_shape=[jax.ShapeDtypeStruct((heads, row...  2.08 us

profile of v3, /device:TPU:113, one launch (start us, length us, event | category | flops | bytes accessed | tf_op | source)
XLA Modules:
  0.0 61.9 jit_solution(15971609321046289646)
XLA Ops:
  0.6 59.0 %attn_bwd.1.packed = bf16[5,1024,128]{2,1,0:T(8,128)(2,1)} custom-call(bf16[3,1024,128]{2,1,0:T(8,128)(2,1)} %bitcast.5, bf16[3,1024,128]{2,1,0:T(8,128)(2,1)} %bitcast.6, bf16[3,1024,128]{2,1,0:T(8,128)(2,1)} %bitcast.7, f32[3,1024]{1,0:T(4,128)} %bitcast.8, bf16[1024,128]{1,0:T(8,128)(2,1)} %k_hbm.1, bf16[1024,128]{1,0:T(8,128)(2,1)} %v_hbm.1), custom_call_target="tpu_custom_call" | custom-call | tf_op jit(solution)/shard_map/attn_bwd/pallas_call | solution.py:443
  59.6 2.1 %unpack.1 = (bf16[3,1024,128]{2,1,0:T(8,128)(2,1)}, bf16[1024,128]{1,0:T(8,128)(2,1)}, bf16[1024,128]{1,0:T(8,128)(2,1)}) custom-call(bf16[5,1024,128]{2,1,0:T(8,128)(2,1)} %attn_bwd.1.packed), custom_call_target="tpu_custom_call" | custom-call | tf_op jit(solution)/shard_map/unpack/pallas_call | solution.py:472

commit v4 on v3

--- a/solution.py
+++ b/solution.py
@@ -18,11 +18,11 @@
     return lax.dot_general(a, b, dims, preferred_element_type=jnp.float32)
 
 
-def kernel(n_dev, q_hbm, do_hbm, fo_hbm, lse_hbm, k_hbm, v_hbm, out_hbm,
+def kernel(n_dev, n_guest, q_hbm, do_hbm, fo_hbm, lse_hbm, k_hbm, v_hbm, out_hbm,
            q, do, fo, lse, stats, qt, dot_t, lseb, delb, kv, acc, dq, rbuf, rhalf, rdq, out,
            guest_q, guest_do, guest_stats, guest_qt, guest_dot, guest_lse, guest_del, guest_dq, back_dq,
            in_sem, pair_send, pair_recv, kv_send, kv_recv, g_send, g_recv, f_send, d_send, d_recv,
-           guest_send, guest_recv, out_sem):
+           guest_send, guest_recv, back_recv, out_sem):
     heads, rows, dim = q.shape[1:]
     half = rows // 2
     scale = dim ** -0.5
@@ -66,40 +66,60 @@
         return [remote(kv.at[src_slot, i, span], kv.at[slot, i, span],
                        kv_send.at[sem_row, h, i], kv_recv.at[slot, h, i], device) for i in range(2)]
 
-    def kv_send_own(sem_row, to_chip):
-        for h in range(2):
-            for copy in kv_copies(chip, own_slot + core, h, sem_row, at(to_chip)):
-                copy.start()
-
-    def kv_wait_sent(sem_row):
-        for h in range(2):
-            for copy in kv_copies(0, 0, h, sem_row, at(chip)):
+    def give_kv(to_chip, h):
+        for copy in kv_copies(chip, own_slot + core, h, to_chip - 1, at(to_chip)):
+            copy.start()
+
+    def kv_sent(row):
+        for h in range(2):
+            for copy in kv_copies(0, 0, h, row, at(chip)):
                 copy.wait_send()
 
-    late_next = jnp.logical_and(chip == last - 1, core == 0)
-    late_wrap = jnp.logical_and(chip == 0, core == 1)
+    def kv_send_far():
+        for h in range(2):
+            give_kv(last, h)
+
+    first_far = jnp.logical_or(jnp.logical_and(chip == 0, core == 0), jnp.logical_and(chip == last - 1, core == 1))
     loads[0].wait()
     loads[1].wait()
 
-    @pl.when(jnp.logical_and(chip < last, jnp.logical_not(late_next)))
-    def _():
-        kv_send_own(0, chip + 1)
-
-    @pl.when(jnp.logical_and(chip == 0, core == 0))
-    def _():
-        kv_send_own(1, last)
+    @pl.when(first_far)
+    def _():
+        kv_send_far()
+
+    @pl.when(chip == 0)
+    def _():
+        for h in range(2):
+            give_kv(1, h)
+
+        @pl.when(core == 0)
+        def _():
+            for h in range(2):
+                give_kv(2, h)
+
+    @pl.when(chip == 1)
+    def _():
+        for h in range(2):
+            give_kv(2, h)
 
     def pair_copies(c):
         refs = (q.at[c], do.at[c], kv.at[own_slot + c, 0], kv.at[own_slot + c, 1], stats.at[c])
         return [remote(ref, ref, pair_send.at[i], pair_recv.at[i], partner) for i, ref in enumerate(refs)]
 
-    guest_rows = pl.ds(half, half)
-    guests = [
-        remote(q.at[core, :, guest_rows], guest_q, guest_send.at[0], guest_recv.at[0], at(0)),
-        remote(do.at[core, :, guest_rows], guest_do, guest_send.at[1], guest_recv.at[1], at(0)),
-        remote(stats.at[core, :, guest_rows], guest_stats, guest_send.at[2], guest_recv.at[2], at(0)),
-    ]
-    guests_back = remote(guest_dq, back_dq, d_send.at[2], d_recv.at[2], at(last))
+    def guest_copies(to_chip):
+        n = n_guest[to_chip]
+        src, dst = pl.ds(rows - n, n), pl.ds(0, n)
+        pairs = ((q.at[core, :, src], guest_q.at[:, dst]), (do.at[core, :, src], guest_do.at[:, dst]),
+                 (stats.at[core, :, src], guest_stats.at[:, dst]))
+        return [remote(src, dst, guest_send.at[to_chip, i], guest_recv.at[i], at(to_chip))
+                for i, (src, dst) in enumerate(pairs)]
+
+    guests = [guest_copies(to_chip) for to_chip in range(2)]
+
+    def guests_back(from_chip):
+        span = pl.ds(0, n_guest[from_chip])
+        return remote(guest_dq.at[:, span], back_dq.at[from_chip, :, span],
+                      d_send.at[2], back_recv.at[from_chip], at(last))
 
     pair = pair_copies(core)
     for i in (2, 3):
@@ -107,7 +127,8 @@
 
         @pl.when(chip == last)
         def _():
-            guests[i - 2].start()
+            for copies in guests:
+                copies[i - 2].start()
 
         pair[i - 2].start()
     pair[2].start()
@@ -122,7 +143,8 @@
 
     @pl.when(chip == last)
     def _():
-        guests[2].start()
+        for copies in guests:
+            copies[2].start()
 
     def spread(row):
         return jnp.broadcast_to(row, (dim, row.shape[1])).T
@@ -163,43 +185,64 @@
             n = heads * size
             dq[b, :, first:first + size, :] += d_query[i * n:(i + 1) * n].reshape(heads, size, dim)
 
+    def own_low():
+        tile((core,), half, half, own_slot + core, 0)
+
+    def partner_masked():
+        tile((other,), half, half, own_slot + other, 1, masked=True)
+
+    def square():
+        tile((1,), 0, rows, own_slot, core)
+
     prep(core)
     tile((core,), 0, half, own_slot + core, 0, masked=True)
-    tile((core,), half, half, own_slot + core, 0)
+
+    @pl.when(core == 1)
+    def _():
+        own_low()
 
     for copy in pair_copies(other):
         copy.wait_recv()
 
-    @pl.when(late_wrap)
-    def _():
-        kv_send_own(1, last)
+    @pl.when(jnp.logical_and(chip == 0, core == 1))
+    def _():
+        kv_send_far()
 
     prep(other)
 
-    @pl.when(chip == 0)
-    def _():
-        for copy in guests:
+    @pl.when(core == 0)
+    def _():
+        partner_masked()
+
+    def host(to_chip):
+        for copy in guests[to_chip]:
             copy.wait_recv()
-        n = heads * half
-        guest_qt[...] = guest_q[...].reshape(n, dim).T
-        guest_dot[...] = guest_do[...].reshape(n, dim).T
+        size = n_guest[to_chip]
+        n = heads * size
+        flat = lambda ref: ref[:, :size, :].reshape(n, dim)
+        guest_qt[:, :n] = flat(guest_q).T
+        guest_dot[:, :n] = flat(guest_do).T
         for g in range(heads):
-            guest_lse[g] = spread(guest_stats[g:g + 1, :])
-            guest_del[g] = spread(guest_stats[heads + g:heads + g + 1, :])
-        guest_dq[...] = jnp.zeros_like(guest_dq)
+            guest_lse[g, :size] = spread(guest_stats[g:g + 1, :size])
+            guest_del[g, :size] = spread(guest_stats[heads + g:heads + g + 1, :size])
+        guest_dq[:, :size] = jnp.zeros((heads, size, dim), jnp.float32)
 
         @pl.loop(0, 2)
         def _(b):
-            flat = lambda ref: ref[...].reshape(n, dim)
             d_key, d_value, d_query = pair_grads(
-                flat(guest_q), flat(guest_do), guest_qt[...], guest_dot[...], flat(guest_lse), flat(guest_del),
-                kv[own_slot + b, 0], kv[own_slot + b, 1], half, False)
+                flat(guest_q), flat(guest_do), guest_qt[:, :n], guest_dot[:, :n], flat(guest_lse), flat(guest_del),
+                kv[own_slot + b, 0], kv[own_slot + b, 1], size, False)
             for h in range(2):
                 acc[own_slot + b, h, 0] += d_key[:, h * half:(h + 1) * half]
                 acc[own_slot + b, h, 1] += d_value[:, h * half:(h + 1) * half]
-            guest_dq[...] += d_query.reshape(heads, half, dim)
-
-        guests_back.start()
+            guest_dq[:, :size] += d_query.reshape(heads, size, dim)
+
+        guests_back(to_chip).start()
+
+    for to_chip in range(2):
+        @pl.when(chip == to_chip)
+        def _():
+            host(to_chip)
 
     def g_copy(slot, h, buf, to_chip):
         return remote(acc.at[slot, h], rbuf.at[buf, h], g_send.at[slot, h], g_recv.at[buf, h], at(to_chip))
@@ -253,37 +296,60 @@
             def _():
                 g_copy(slot, h, A, 2).start()
 
-    @pl.loop(0, chip)
-    def _(t):
-        slot = jnp.where(jnp.logical_and(chip == last, core == 0), t, chip - 1 - t)
-
-        @pl.loop(0, 2)
-        def _(h):
-            for copy in kv_copies(slot, own_slot + core, h, 0, at(chip)):
+    @pl.loop(0, 2 * chip)
+    def _(u):
+        near_first = jnp.where(jnp.logical_and(chip == last, core == 0), u // 2, chip - 1 - u // 2)
+        far_inside = chip == last - 1
+        inside = jnp.logical_and(far_inside, core == 0)
+        slot = jnp.where(inside, jnp.where(jnp.logical_or(u == 0, u == 3), 1, 0), near_first)
+        h = jnp.where(inside, u // 2, u % 2)
+
+        def arrived(from_slot, part):
+            for copy in kv_copies(from_slot, own_slot + core, part, 0, at(chip)):
                 copy.wait_recv()
 
-            @pl.when(jnp.logical_and(chip < last, slot == chip - 1))
-            def _():
-                for copy in kv_copies(slot, slot, h, 2, at(chip + 1)):
-                    copy.start()
-
-                @pl.when(jnp.logical_and(late_next, h == 1))
-                def _():
-                    kv_send_own(0, chip + 1)
-
-            with_guests = jnp.logical_and(chip == last, slot == 0)
-
-            @pl.when(with_guests)
-            def _():
-                tile((0, 1), 0, half, slot, h)
-
-            @pl.when(jnp.logical_not(with_guests))
+        def pass_on(from_slot, part, to_chip):
+            for copy in kv_copies(from_slot, from_slot, part, from_slot, at(to_chip)):
+                copy.start()
+
+        awaited_before = jnp.logical_and(far_inside, jnp.logical_and(slot == 1, h == 1))
+
+        @pl.when(jnp.logical_and(far_inside, u == 1))
+        def _():
+            arrived(1, 1)
+            pass_on(1, 1, last)
+
+        @pl.when(jnp.logical_not(awaited_before))
+        def _():
+            arrived(slot, h)
+
+        @pl.when(jnp.logical_and(far_inside, u == 0))
+        def _():
+            pass_on(1, 0, last)
+
+            @pl.when(core == 0)
+            def _():
+                kv_send_far()
+
+        @pl.when(jnp.logical_and(chip == 1, core == 1))
+        def _():
+            pass_on(slot, h, 2)
+
+        without_guests = jnp.logical_and(chip == last, slot < 2)
+        for to_chip in range(2):
+            @pl.when(jnp.logical_and(chip == last, slot == to_chip))
             def _():
                 @pl.loop(0, 2)
                 def _(b):
-                    tile((b,), 0, rows, slot, h)
-
-            send_partial(slot, h)
+                    tile((b,), 0, rows - n_guest[to_chip], slot, h)
+
+        @pl.when(jnp.logical_not(without_guests))
+        def _():
+            @pl.loop(0, 2)
+            def _(b):
+                tile((b,), 0, rows, slot, h)
+
+        send_partial(slot, h)
 
     relay_add = jnp.logical_and(jnp.logical_or(chip == 1, chip == 2), core == 0)
     relay_pass = jnp.logical_and(chip == 0, core == 1)
@@ -302,28 +368,29 @@
     give_dq = remote(dq.at[other], rdq, d_send.at[1], d_recv.at[1], partner)
 
     relay(0)
-    tile((other,), half, half, own_slot + other, 1, masked=True)
 
     @pl.when(core == 0)
     def _():
         swaps[1].start()
+        square()
 
     @pl.when(core == 1)
     def _():
-        give_dq.start()
-
+        partner_masked()
+
+    give_dq.start()
     relay(1)
-    tile((1,), 0, rows, own_slot, core)
+
+    @pl.when(core == 0)
+    def _():
+        own_low()
 
     @pl.when(core == 1)
     def _():
+        square()
         swaps[1].start()
 
-    @pl.when(core == 0)
-    def _():
-        give_dq.start()
-
-    @pl.when(chip == 0)
+    @pl.when(chip < 2)
     def _():
         swaps[0].start()
 
@@ -333,9 +400,15 @@
 
     @pl.when(chip == last)
     def _():
-        guests_back.wait_recv()
+        for from_chip in range(2):
+            guests_back(from_chip).wait_recv()
         for g in range(heads):
-            out[g, half:, :] = ((dq[core, g, half:, :] + rdq[g, half:, :] + back_dq[g]) * scale).astype(out.dtype)
+            for n in (n_guest[0], n_guest[1]):
+                first = rows - n
+                total = dq[core, g, first:, :] + rdq[g, first:, :] + back_dq[0, g, n_guest[0] - n:, :]
+                if n == n_guest[1]:
+                    total = total + back_dq[1, g, :n, :]
+                out[g, first:, :] = (total * scale).astype(out.dtype)
 
     stores = [pltpu.make_async_copy(out.at[0:heads], out_hbm.at[0:heads], out_sem.at[0])]
     for h in range(2):
@@ -351,7 +424,7 @@
             g_wait(R, h)
             pass_copy(h).start()
 
-    @pl.when(chip == 0)
+    @pl.when(chip < 2)
     def _():
         swaps[0].wait_recv()
         acc[own_slot + core, 0] += rhalf[0]
@@ -380,24 +453,32 @@
     give_dq.wait_send()
     swaps[1].wait_send()
 
-    @pl.when(chip == 0)
+    @pl.when(chip < 2)
     def _():
         swaps[0].wait_send()
-        guests_back.wait_send()
-        kv_wait_sent(1)
+
+    for from_chip in range(2):
+        @pl.when(chip == from_chip)
+        def _():
+            guests_back(from_chip).wait_send()
 
     @pl.when(chip == last)
     def _():
-        for copy in guests:
-            copy.wait_send()
-
-    @pl.when(chip < last)
-    def _():
-        kv_wait_sent(0)
-
-    @pl.when(jnp.logical_and(chip >= 1, chip < last))
-    def _():
-        kv_wait_sent(2)
+        for copies in guests:
+            for copy in copies:
+                copy.wait_send()
+
+    @pl.when(jnp.logical_or(chip == 0, chip == last - 1))
+    def _():
+        kv_sent(last - 1)
+
+    @pl.when(jnp.logical_and(chip < last, me != 1))
+    def _():
+        kv_sent(1)
+
+    @pl.when(jnp.logical_or(chip == 0, me == 3))
+    def _():
+        kv_sent(0)
 
     @pl.loop(0, chip)
     def _(slot):
@@ -435,13 +516,15 @@
     def local_fn(q_tok, k_tok, v_tok, fwd_out, d_out, lse_row):
         rows, heads, dim = q_tok.shape
         half = rows // 2
+        n_guest = (3 * rows // 8, rows // 4)
+        most = max(n_guest)
         n_slot = n_dev // 2 + 2
         bf16, f32 = jnp.bfloat16, jnp.float32
         any_spec = pl.BlockSpec(memory_space=pl.ANY)
         dma = pltpu.SemaphoreType.DMA
         vmem = pltpu.VMEM
         packed = pl.pallas_call(
-            functools.partial(kernel, n_dev),
+            functools.partial(kernel, n_dev, n_guest),
             out_shape=jax.ShapeDtypeStruct((heads + 2, rows, dim), bf16),
             in_specs=[any_spec] * 6,
             out_specs=any_spec,
@@ -456,14 +539,14 @@
                 vmem((3, 2, 2, dim, half), f32), vmem((2, 2, dim, half), f32),
                 vmem((heads, rows, dim), f32),
                 vmem((heads + 2, rows, dim), bf16),
-                vmem((heads, half, dim), bf16), vmem((heads, half, dim), bf16), vmem((8, half), f32),
-                vmem((dim, heads * half), bf16), vmem((dim, heads * half), bf16),
-                vmem((heads, half, dim), f32), vmem((heads, half, dim), f32),
-                vmem((heads, half, dim), f32), vmem((heads, half, dim), f32),
+                vmem((heads, most, dim), bf16), vmem((heads, most, dim), bf16), vmem((8, most), f32),
+                vmem((dim, heads * most), bf16), vmem((dim, heads * most), bf16),
+                vmem((heads, most, dim), f32), vmem((heads, most, dim), f32),
+                vmem((heads, most, dim), f32), vmem((2, heads, most, dim), f32),
                 dma((6,)), dma((5,)), dma((5,)),
                 dma((3, 2, 2)), dma((n_slot, 2, 2)),
                 dma((n_slot, 2)), dma((3, 2)), dma((2,)), dma((4,)), dma((4,)),
-                dma((3,)), dma((3,)), dma((5,)),
+                dma((2, 3)), dma((3,)), dma((2,)), dma((5,)),
             ],
             compiler_params=pltpu.CompilerParams(
                 collective_id=0, has_side_effects=True, vmem_limit_bytes=62 * 2 ** 20),

time: 63.1 us -> 60.4 us (0.957); the launches traced: 61.9 us -> 60.3 us
  Pallas kernels: 61.1 us -> 59.5 us
    pallas_call x1, Pallas kernels: 59 us -> 57.4 us  [local_fn(): pl.pallas_call(functools.partial(kernel, n_dev, n_guest), out_shape=jax.S...]
where the time goes in v4:
time: 60.4 us; the launch traced here: 60.3 us
  Pallas kernels  59.5 us (99%)
  between operations  0.82 us (1%)
    pallas_call x1, Pallas kernels, local_fn(): pl.pallas_call(functools.partial(kernel, n_dev, n_guest), out_shape=jax.S...  57.4 us
    pallas_call x1, Pallas kernels, local_fn(): pl.pallas_call(unpack_kernel, out_shape=[jax.ShapeDtypeStruct((heads, row...  2.08 us

profile of v4, /device:TPU:113, one launch (start us, length us, event | category | flops | bytes accessed | tf_op | source)
XLA Modules:
  0.0 60.3 jit_solution(12118335877514060475)
XLA Ops:
  0.6 57.4 %attn_bwd.1.packed = bf16[5,1024,128]{2,1,0:T(8,128)(2,1)} custom-call(bf16[3,1024,128]{2,1,0:T(8,128)(2,1)} %bitcast.5, bf16[3,1024,128]{2,1,0:T(8,128)(2,1)} %bitcast.6, bf16[3,1024,128]{2,1,0:T(8,128)(2,1)} %bitcast.7, f32[3,1024]{1,0:T(4,128)} %bitcast.8, bf16[1024,128]{1,0:T(8,128)(2,1)} %k_hbm.1, bf16[1024,128]{1,0:T(8,128)(2,1)} %v_hbm.1), custom_call_target="tpu_custom_call" | custom-call | tf_op jit(solution)/shard_map/attn_bwd/pallas_call | solution.py:526
  58.0 2.1 %unpack.1 = (bf16[3,1024,128]{2,1,0:T(8,128)(2,1)}, bf16[1024,128]{1,0:T(8,128)(2,1)}, bf16[1024,128]{1,0:T(8,128)(2,1)}) custom-call(bf16[5,1024,128]{2,1,0:T(8,128)(2,1)} %attn_bwd.1.packed), custom_call_target="tpu_custom_call" | custom-call | tf_op jit(solution)/shard_map/unpack/pallas_call | solution.py:555

commit v5 on v4

--- a/solution.py
+++ b/solution.py
@@ -18,11 +18,11 @@
     return lax.dot_general(a, b, dims, preferred_element_type=jnp.float32)
 
 
-def kernel(n_dev, n_guest, q_hbm, do_hbm, fo_hbm, lse_hbm, k_hbm, v_hbm, out_hbm,
-           q, do, fo, lse, stats, qt, dot_t, lseb, delb, kv, acc, dq, rbuf, rhalf, rdq, out,
+def kernel(n_dev, n_guest, q_hbm, do_hbm, fo_hbm, lse_hbm, k_hbm, v_hbm, out,
+           q, do, fo, lse, stats, qt, dot_t, lseb, delb, kv, acc, dq, rbuf, rhalf, rdq,
            guest_q, guest_do, guest_stats, guest_qt, guest_dot, guest_lse, guest_del, guest_dq, back_dq,
            in_sem, pair_send, pair_recv, kv_send, kv_recv, g_send, g_recv, f_send, d_send, d_recv,
-           guest_send, guest_recv, back_recv, out_sem):
+           guest_send, guest_recv, back_recv):
     heads, rows, dim = q.shape[1:]
     half = rows // 2
     scale = dim ** -0.5
@@ -410,14 +410,6 @@
                     total = total + back_dq[1, g, :n, :]
                 out[g, first:, :] = (total * scale).astype(out.dtype)
 
-    stores = [pltpu.make_async_copy(out.at[0:heads], out_hbm.at[0:heads], out_sem.at[0])]
-    for h in range(2):
-        span = pl.ds(h * half, half)
-        for i in range(2):
-            stores.append(pltpu.make_async_copy(
-                out.at[heads + i, span], out_hbm.at[heads + i, span], out_sem.at[1 + 2 * h + i]))
-    stores[0].start()
-
     @pl.when(relay_pass)
     def _():
         for h in range(2):
@@ -445,8 +437,6 @@
 
         out[heads, h * half:(h + 1) * half, :] = (acc[own_slot + core, h, 0].T * scale).astype(out.dtype)
         out[heads + 1, h * half:(h + 1) * half, :] = acc[own_slot + core, h, 1].T.astype(out.dtype)
-        stores[1 + 2 * h].start()
-        stores[2 + 2 * h].start()
 
     for copy in pair:
         copy.wait_send()
@@ -490,21 +480,14 @@
         for h in range(2):
             pass_copy(h).wait_send()
 
-    for copy in stores:
-        copy.wait()
-
-
-def unpack_kernel(packed, gq, gk, gv, held, in_sem, out_sem):
+
+def unpack_kernel(packed, gq, gk, gv, out_sem):
     heads = gq.shape[0]
-    n = packed.shape[0]
-    reads = [pltpu.make_async_copy(packed.at[i], held.at[i], in_sem.at[i]) for i in range(n)]
-    outs = [gq.at[i] for i in range(heads)] + [gk, gv]
-    writes = [pltpu.make_async_copy(held.at[i], outs[i], out_sem.at[i]) for i in range(n)]
-    for copy in reads:
+    outs = [gq, gk, gv]
+    parts = [packed.at[0:heads], packed.at[heads], packed.at[heads + 1]]
+    writes = [pltpu.make_async_copy(part, dst, out_sem.at[i]) for i, (part, dst) in enumerate(zip(parts, outs))]
+    for copy in writes:
         copy.start()
-    for read, write in zip(reads, writes):
-        read.wait()
-        write.start()
     for copy in writes:
         copy.wait()
 
@@ -525,9 +508,9 @@
         vmem = pltpu.VMEM
         packed = pl.pallas_call(
             functools.partial(kernel, n_dev, n_guest),
-            out_shape=jax.ShapeDtypeStruct((heads + 2, rows, dim), bf16),
+            out_shape=vmem((heads + 2, rows, dim), bf16),
             in_specs=[any_spec] * 6,
-            out_specs=any_spec,
+            out_specs=pl.BlockSpec(memory_space=vmem),
             scratch_shapes=[
                 vmem((2, heads, rows, dim), bf16), vmem((2, heads, rows, dim), bf16),
                 vmem((heads, rows, dim), bf16), vmem((heads, rows), f32), vmem((2, 8, rows), f32),
@@ -538,7 +521,6 @@
                 vmem((2, heads, rows, dim), f32),
                 vmem((3, 2, 2, dim, half), f32), vmem((2, 2, dim, half), f32),
                 vmem((heads, rows, dim), f32),
-                vmem((heads + 2, rows, dim), bf16),
                 vmem((heads, most, dim), bf16), vmem((heads, most, dim), bf16), vmem((8, most), f32),
                 vmem((dim, heads * most), bf16), vmem((dim, heads * most), bf16),
                 vmem((heads, most, dim), f32), vmem((heads, most, dim), f32),
@@ -546,10 +528,10 @@
                 dma((6,)), dma((5,)), dma((5,)),
                 dma((3, 2, 2)), dma((n_slot, 2, 2)),
                 dma((n_slot, 2)), dma((3, 2)), dma((2,)), dma((4,)), dma((4,)),
-                dma((2, 3)), dma((3,)), dma((2,)), dma((5,)),
+                dma((2, 3)), dma((3,)), dma((2,)),
             ],
             compiler_params=pltpu.CompilerParams(
-                collective_id=0, has_side_effects=True, vmem_limit_bytes=62 * 2 ** 20),
+                collective_id=0, has_side_effects=True, vmem_limit_bytes=56 * 2 ** 20),
             name='attn_bwd',
         )(q_tok.transpose(1, 0, 2), d_out.transpose(1, 0, 2), fwd_out.transpose(1, 0, 2), lse_row.T, k_tok, v_tok)
         gq, gk, gv = pl.pallas_call(
@@ -559,11 +541,11 @@
                 jax.ShapeDtypeStruct((rows, dim), bf16),
                 jax.ShapeDtypeStruct((rows, dim), bf16),
             ],
-            in_specs=[any_spec],
+            in_specs=[pl.BlockSpec(memory_space=vmem)],
             out_specs=[any_spec] * 3,
-            scratch_shapes=[pltpu.VMEM((heads + 2, rows, dim), bf16), dma((heads + 2,)), dma((heads + 2,))],
+            scratch_shapes=[dma((3,))],
             name='unpack',
-        )(packed)
+        )(pltpu.with_memory_space_constraint(packed, pltpu.VMEM))
         return gq.transpose(1, 0, 2), gk, gv
 
     return jax.shard_map(local_fn, mesh=mesh, in_specs=(row_spec,) * 6, out_specs=(row_spec,) * 3, check_vma=False)

time: 60.4 us -> 58.7 us (0.972)
  Pallas kernels: 59.5 us -> 57.8 us
    pallas_call x1, Pallas kernels: 2.08 us -> 1.08 us  [local_fn(): pl.pallas_call(unpack_kernel, out_shape=[jax.ShapeDtypeStruct((heads, row...]
    pallas_call x1, Pallas kernels: 57.4 us -> 56.7 us  [local_fn(): pl.pallas_call(functools.partial(kernel, n_dev, n_guest), out_shape=vmem(...]
where the time goes in v5:
time: 58.7 us; the launch traced here: 58.6 us
  Pallas kernels  57.8 us (98%)
  between operations  0.82 us (1%)
    pallas_call x1, Pallas kernels, local_fn(): pl.pallas_call(functools.partial(kernel, n_dev, n_guest), out_shape=vmem(...  56.7 us

profile of v5, /device:TPU:113, one launch (start us, length us, event | category | flops | bytes accessed | tf_op | source)
XLA Modules:
  0.0 58.6 jit_solution(13022838179859985719)
XLA Ops:
  0.6 56.7 %attn_bwd.1.packed = bf16[5,1024,128]{2,1,0:T(8,128)(2,1)S(1)} custom-call(bf16[3,1024,128]{2,1,0:T(8,128)(2,1)} %bitcast.5, bf16[3,1024,128]{2,1,0:T(8,128)(2,1)} %bitcast.6, bf16[3,1024,128]{2,1,0:T(8,128)(2,1)} %bitcast.7, f32[3,1024]{1,0:T(4,128)} %bitcast.8, bf16[1024,128]{1,0:T(8,128)(2,1)} %k_hbm.1, bf16[1024,128]{1,0:T(8,128)(2,1)} %v_hbm.1), custom_call_target="tpu_custom_call" | custom-call | tf_op jit(solution)/shard_map/attn_bwd/pallas_call | solution.py:509
  57.3 1.1 %unpack.1 = (bf16[3,1024,128]{2,1,0:T(8,128)(2,1)}, bf16[1024,128]{1,0:T(8,128)(2,1)}, bf16[1024,128]{1,0:T(8,128)(2,1)}) custom-call(bf16[5,1024,128]{2,1,0:T(8,128)(2,1)S(1)} %attn_bwd.1.packed), custom_call_target="tpu_custom_call" | custom-call | tf_op jit(solution)/shard_map/unpack/pallas_call | solution.py:537

commit v6 on v5

--- a/solution.py
+++ b/solution.py
@@ -239,6 +239,22 @@
 
         guests_back(to_chip).start()
 
+    def arrived(from_slot, part):
+        for copy in kv_copies(from_slot, own_slot + core, part, 0, at(chip)):
+            copy.wait_recv()
+
+    def pass_on(from_slot, part, to_chip):
+        for copy in kv_copies(from_slot, from_slot, part, from_slot, at(to_chip)):
+            copy.start()
+
+    relays_kv = jnp.logical_and(chip == 1, core == 1)
+
+    @pl.when(relays_kv)
+    def _():
+        for part in range(2):
+            arrived(0, part)
+            pass_on(0, part, 2)
+
     for to_chip in range(2):
         @pl.when(chip == to_chip)
         def _():
@@ -304,15 +320,7 @@
         slot = jnp.where(inside, jnp.where(jnp.logical_or(u == 0, u == 3), 1, 0), near_first)
         h = jnp.where(inside, u // 2, u % 2)
 
-        def arrived(from_slot, part):
-            for copy in kv_copies(from_slot, own_slot + core, part, 0, at(chip)):
-                copy.wait_recv()
-
-        def pass_on(from_slot, part, to_chip):
-            for copy in kv_copies(from_slot, from_slot, part, from_slot, at(to_chip)):
-                copy.start()
-
-        awaited_before = jnp.logical_and(far_inside, jnp.logical_and(slot == 1, h == 1))
+        awaited_before = jnp.logical_or(relays_kv, jnp.logical_and(far_inside, jnp.logical_and(slot == 1, h == 1)))
 
         @pl.when(jnp.logical_and(far_inside, u == 1))
         def _():
@@ -330,10 +338,6 @@
             @pl.when(core == 0)
             def _():
                 kv_send_far()
-
-        @pl.when(jnp.logical_and(chip == 1, core == 1))
-        def _():
-            pass_on(slot, h, 2)
 
         without_guests = jnp.logical_and(chip == last, slot < 2)
         for to_chip in range(2):

time: 58.7 us -> 58.6 us (level); the launches traced: 58.6 us -> 57.8 us
  Pallas kernels: 57.8 us -> 57 us
    pallas_call x1, Pallas kernels: 56.7 us -> 56 us  [local_fn(): pl.pallas_call(functools.partial(kernel, n_dev, n_guest), out_shape=vmem(...]
where the time goes in v6:
time: 58.6 us; the launch traced here: 57.8 us
  Pallas kernels  57 us (97%)
  between operations  0.82 us (1%)
    pallas_call x1, Pallas kernels, local_fn(): pl.pallas_call(functools.partial(kernel, n_dev, n_guest), out_shape=vmem(...  56 us

profile of v6, /device:TPU:113, one launch (start us, length us, event | category | flops | bytes accessed | tf_op | source)
XLA Modules:
  0.0 57.8 jit_solution(109537313732770097)
XLA Ops:
  0.6 56.0 %attn_bwd.1.packed = bf16[5,1024,128]{2,1,0:T(8,128)(2,1)S(1)} custom-call(bf16[3,1024,128]{2,1,0:T(8,128)(2,1)} %bitcast.5, bf16[3,1024,128]{2,1,0:T(8,128)(2,1)} %bitcast.6, bf16[3,1024,128]{2,1,0:T(8,128)(2,1)} %bitcast.7, f32[3,1024]{1,0:T(4,128)} %bitcast.8, bf16[1024,128]{1,0:T(8,128)(2,1)} %k_hbm.1, bf16[1024,128]{1,0:T(8,128)(2,1)} %v_hbm.1), custom_call_target="tpu_custom_call" | custom-call | tf_op jit(solution)/shard_map/attn_bwd/pallas_call | solution.py:513
  56.6 1.1 %unpack.1 = (bf16[3,1024,128]{2,1,0:T(8,128)(2,1)}, bf16[1024,128]{1,0:T(8,128)(2,1)}, bf16[1024,128]{1,0:T(8,128)(2,1)}) custom-call(bf16[5,1024,128]{2,1,0:T(8,128)(2,1)S(1)} %attn_bwd.1.packed), custom_call_target="tpu_custom_call" | custom-call | tf_op jit(solution)/shard_map/unpack/pallas_call | solution.py:541
